TPU v7x, 32 devices: a whole 2x2x4 slice. The times are simulated.
32 devices in a mesh: dp: 8 (over z, y), tensor: 4 (over x, core).
Axes of the slice: x: 2, y: 2, z: 4, core: 2. Of those that a mesh axis runs over, the one named last changes fastest.
Arguments:
- tokens: bfloat16 [2048, 2048], P('dp'), may hold values from -6 to 6
- qkv_weight: bfloat16 [2048, 3, 2048], P('dp', None, 'tensor'), may hold values from -0.13258252 to 0.13258252
- out_weight: bfloat16 [2048, 2048], P('dp', 'tensor'), may hold values from -0.125 to 0.125
- gu_weight: bfloat16 [2048, 2, 8192], P('dp', None, 'tensor'), may hold values from -0.125 to 0.125
- down_weight: bfloat16 [2048, 8192], P('dp', 'tensor'), may hold values from -0.0625 to 0.0625
- attn_gain: bfloat16 [2048], P('dp'), may hold values from 0.25 to 1.75
- ffn_gain: bfloat16 [2048], P('dp'), may hold values from 0.25 to 1.75
- q_gain: bfloat16 [2048], P(('tensor', 'dp')), may hold values from 0.5 to 5
- k_gain: bfloat16 [2048], P(('tensor', 'dp')), may hold values from 0.5 to 5
- out_grad: float32 [2048, 2048], P('dp'), may hold values from -6 to 6
Outputs:
- block_out: float32 [2048, 2048], P('dp')
- grad_tokens: float32 [2048, 2048], P('dp')
- grad_qkv_weight: float32 [2048, 3, 2048], P('dp', None, 'tensor')
- grad_out_weight: float32 [2048, 2048], P('dp', 'tensor')
- grad_gu_weight: float32 [2048, 2, 8192], P('dp', None, 'tensor')
- grad_down_weight: float32 [2048, 8192], P('dp', 'tensor')
- grad_attn_gain: float32 [2048], P('dp')
- grad_ffn_gain: float32 [2048], P('dp')
- grad_q_gain: float32 [2048], P(('tensor', 'dp'))
- grad_k_gain: float32 [2048], P(('tensor', 'dp'))
All inputs are finite; a program needn't handle non-finite values.
Results may differ from a plain program's by a relative error of at most 0.015.
The roundings to bfloat16 on the way count: a program that leaves them out, or rounds other values in their place, can miss the bound.
Values may be sent and summed in bfloat16 or wider, within the bound.
A program may use at most 256 MiB of HBM per device.

v0:
```python
import functools

import jax
import jax.numpy as jnp
from jax import lax
from jax.experimental import pallas as pl
from jax.experimental.pallas import tpu as pltpu
from jax.sharding import Mesh, PartitionSpec as P

HEADS = 16
HD = 128
SEQ_LEN = 256
HQ = 2048

epsilon = 1e-06
rope_base = 500000.0

f32 = jnp.float32
bf16 = jnp.bfloat16
MESH = pl.DeviceIdType.MESH
EXACT = lax.Precision.HIGHEST
VMEM_LIMIT = 60 * 1024 * 1024
TILE = 32
HALVES = 2


def flip(index, bit):
    return index + bit - 2 * bit * ((index // bit) % 2)


def across(index, k):
    bit = 1
    while bit <= k:
        if k & bit:
            index = flip(index, bit)
        bit *= 2
    return index


def exclusive_or(left, right, count):
    total, bit = 0, 1
    while bit < count:
        total = total + bit * ((left // bit + right // bit) % 2)
        bit *= 2
    return total


def pick(operand, index, axis):
    return lax.dynamic_index_in_dim(operand, index, axis, keepdims=False)


def span(index, size):
    return pl.ds(pl.multiple_of(index * size, size), size)


class Links:
    def __init__(self, send_sem, recv_sem):
        self.send_sem, self.recv_sem, self.count = send_sem, recv_sem, 0
        self.copies, self.lines = [], []

    def send(self, source, target, device):
        copy = self.copy(self.count, source, target, device)
        copy.start()
        self.count += 1
        self.copies.append(copy)
        return copy

    def reserve(self, number):
        self.count += number
        return self.count - number

    def copy(self, index, source, target, device):
        return pltpu.make_async_remote_copy(
            src_ref=source,
            dst_ref=target,
            send_sem=self.send_sem.at[index],
            recv_sem=self.recv_sem.at[index],
            device_id=device,
            device_id_type=MESH,
        )

    def sent(self, copies):
        done = [id(copy) for copy in copies]
        for copy in self.copies:
            if id(copy) in done:
                copy.wait_send()
        self.copies = [copy for copy in self.copies if id(copy) not in done]

    def finish(self):
        for copy in self.copies:
            copy.wait_send()
        for line in self.lines:
            line.finish()


def greet(peers):
    barrier = pltpu.get_barrier_semaphore()
    for peer in peers:
        pl.semaphore_signal(barrier, inc=1, device_id=peer, device_id_type=MESH)
    pl.semaphore_wait(barrier, len(peers))


def fold(block):
    total = block[:, :128]
    for i in range(1, block.shape[1] // 128):
        total = total + block[:, i * 128 : (i + 1) * 128]
    return total


def wide(column, width):
    return jnp.concatenate([column] * (width // 128), axis=1)


def row_mask(row):
    return (lax.broadcasted_iota(jnp.int32, (8, 128), 0) == row).astype(f32)


def to_row(block, row):
    return lax.dot_general(
        row_mask(row), block, (((1,), (1,)), ((), ())), precision=EXACT, preferred_element_type=f32
    )


def to_column(stats, row):
    return lax.dot_general(
        stats, row_mask(row), (((0,), (0,)), ((), ())), precision=EXACT, preferred_element_type=f32
    )


def dot(left, right):
    return jnp.dot(left, right, preferred_element_type=f32)


def dot_t(left, right):
    return lax.dot_general(left, right, (((1,), (1,)), ((), ())), preferred_element_type=f32)


def t_dot(left, right):
    return lax.dot_general(left, right, (((0,), (0,)), ((), ())), preferred_element_type=f32)


def rotate(operand):
    half = HD // 2
    return jnp.concatenate([-operand[:, half:], operand[:, :half]], axis=1)


def rotate_back(operand):
    half = HD // 2
    return jnp.concatenate([operand[:, half:], -operand[:, :half]], axis=1)


def attention(k, qkv, stats, gain_ref, cos_ref, sin_ref):
    stats = stats / HQ
    q_inv = lax.rsqrt(to_column(stats, 2 * k) + epsilon)
    k_inv = lax.rsqrt(to_column(stats, 2 * k + 1) + epsilon)
    queries, key_rows = qkv[:, :HD], qkv[:, HD : 2 * HD]
    values = qkv[:, 2 * HD :].astype(bf16)
    cos_table, sine_table = cos_ref[...], sin_ref[...]
    q_normed = queries * q_inv * gain_ref[0:1]
    k_normed = key_rows * k_inv * gain_ref[1:2]
    q_rot = (q_normed * cos_table + rotate(q_normed) * sine_table).astype(bf16)
    k_rot = (k_normed * cos_table + rotate(k_normed) * sine_table).astype(bf16)
    scores = dot_t(q_rot, k_rot) * HD ** (-0.5)
    ahead = lax.broadcasted_iota(jnp.int32, scores.shape, 1) > lax.broadcasted_iota(
        jnp.int32, scores.shape, 0
    )
    scores = jnp.where(ahead, -1e30, scores)
    shifted = jnp.exp(scores - jnp.max(scores, axis=1, keepdims=True))
    probs = shifted / jnp.sum(shifted, axis=1, keepdims=True)
    return queries, key_rows, values, q_inv, k_inv, q_rot, k_rot, probs


def weight_grad(left, right, out, block, columns=None):
    na, nb, rows = left.shape[0], out.shape[1], out.shape[2]
    columns = columns or slice(0, right.shape[2])
    size = max(rows, 256)


    def chunk(i, carry):
        at = span(block * (nb * rows // size) + i, size)
        total = t_dot(left[0, :, at], right[0])
        for k in range(1, na):
            total = total + t_dot(left[k, :, at], right[k])
        for j in range(size // rows):
            part = total[j * rows : (j + 1) * rows].astype(bf16)
            out[block, i * (size // rows) + j, :, columns] = part
        return carry

    lax.fori_loop(0, nb * rows // size, chunk, 0)


def exchange_b(links, grad, held, columns):
    b = lax.axis_index("b")
    return [
        links.send(
            grad.at[:, across(b, j), :, columns], held.at[j - 1, :, :, columns], {"b": across(b, j)}
        )
        for j in range(1, held.shape[0] + 1)
    ]


def sum_b(copies, own, held, out, columns):
    for copy in copies:
        copy.wait_recv()

    def add(block, carry):
        total = own(block)[:, columns].astype(f32)
        for j in range(held.shape[0]):
            total = total + held[j, block, :, columns].astype(f32)
        out[block, :, columns] = total.astype(bf16)
        return carry

    lax.fori_loop(0, held.shape[1], add, 0)


class Line:
    def __init__(self, links, na, block, own):
        self.links, self.na, self.block, self.own = links, na, block, own
        self.a, self.p = lax.axis_index("a"), lax.axis_index("p")
        self.hop_base = {1: links.reserve(na - 1), -1: links.reserve(na - 1)}
        self.pass_base = links.reserve(na)
        links.lines.append(self)

    def hop(self, way, t):
        a, na = self.a, self.na
        first = a - way * (t - 1)
        source = self.own if t == 1 else self.block(exclusive_or(first, a, na))
        target = self.block(exclusive_or(first, a + way, na))
        return self.links.copy(self.hop_base[way] + t - 1, source, target, {"a": (a + way) % na})

    def sends(self, way, t):
        first, last = self.a - way * (t - 1), self.a + way
        return (first >= 0) & (first < self.na) & (last >= 0) & (last < self.na)

    def to_pair(self, k, source=None):
        at = self.block(k)
        return self.links.copy(self.pass_base + k, at if source is None else source, at, {"p": 1 - self.p})

    def start(self):
        for way in (1, -1):

            @pl.when(self.sends(way, 1))
            def _(way=way):
                self.hop(way, 1).start()

    def pass_on(self, way, t):
        came = self.a - way * t

        @pl.when((came >= 0) & (came < self.na))
        def _():
            self.hop(way, t).wait_recv()
            self.to_pair(exclusive_or(came, self.a, self.na)).start()

        if t < self.na - 1:

            @pl.when(self.sends(way, t + 1))
            def _():
                self.hop(way, t + 1).start()

    def finish(self):
        for way in (1, -1):
            for t in range(1, self.na):

                @pl.when(self.sends(way, t))
                def _(way=way, t=t):
                    self.hop(way, t).wait_send()

        for k in range(self.na):
            self.to_pair(k).wait_send()


class Reduce:
    def __init__(self, na, links, part, out, scratch):
        self.na, self.links, self.part, self.out = na, links, part, out
        self.from_q, self.half_sum, self.from_p, self.to_a, self.from_a = scratch[:5]
        self.total, self.parts, self.cols, self.stat = scratch[5:9]
        self.a, self.p, self.q = (lax.axis_index(axis) for axis in ("a", "p", "q"))
        self.rows, self.width = out.shape[1:]
        self.quarter, self.half = self.width // 4, self.width // 2
        self.count = self.rows // HALVES
        self.mine, self.pair = span(2 * self.q + self.p, self.quarter), span(self.q, self.half)
        self.lead = list(range(2, na)) + [1, 0]
        self.step_q, self.step_p, self.step_a = {}, {}, {}
        self.spread_a, self.spread_p, self.spread_q, self.stats = {}, {}, {}, {}

    def at(self, h):
        return slice(h * self.count, (h + 1) * self.count)

    def each(self, h, body):
        def step(i, carry):
            body(pl.ds(pl.multiple_of(h * self.count + i * TILE, TILE), TILE))
            return carry

        lax.fori_loop(0, self.count // TILE, step, 0)

    def send_q(self, h, k):
        at, q = self.at(h), self.q
        source = self.part.at[k, at, span(1 - q, self.half)]
        self.step_q[h, k] = self.links.send(source, self.from_q.at[k, at], {"q": 1 - q})

    def send_p(self, h, k):
        self.step_q[h, k].wait_recv()

        def add(at):
            own = self.part[k, at, span(self.q, self.half)].astype(f32)
            self.half_sum[k, at] = (own + self.from_q[k, at].astype(f32)).astype(bf16)

        self.each(h, add)
        at, p = self.at(h), self.p
        source = self.half_sum.at[k, at, span(1 - p, self.quarter)]
        self.step_p[h, k] = self.links.send(source, self.from_p.at[k, at], {"p": 1 - p})

    def send_a(self, h, k):
        if not k:
            return
        self.step_p[h, k].wait_recv()

        def add(at):
            own = self.half_sum[k, at, span(self.p, self.quarter)].astype(f32)
            self.to_a[k - 1, at] = (own + self.from_p[k, at].astype(f32)).astype(bf16)

        self.each(h, add)
        at = self.at(h)
        self.step_a[h, k] = self.links.send(
            self.to_a.at[k - 1, at], self.from_a.at[k - 1, at], {"a": across(self.a, k)}
        )

    def add_all(self, at):
        own = self.half_sum[0, at, span(self.p, self.quarter)].astype(f32)
        own = own + self.from_p[0, at].astype(f32)
        for k in range(1, self.na):
            own = own + self.from_a[k - 1, at].astype(f32)
        return own

    def scattered(self, h, first, number):
        self.step_p[h, 0].wait_recv()
        for k in range(1, self.na):
            self.step_a[h, k].wait_recv()
        self.each(h, first)
        if number:
            at = self.at(h)
            stats = to_row(self.parts[0, at], 0)
            if number == 2:
                stats = stats + to_row(self.parts[1, at], 1)
            stat = self.stat
            stat[h, 0] = stats
            self.stats[h] = self.links.send(stat.at[h, 0], stat.at[h, 1], {"p": 1 - self.p})

    def stats_q(self, h):
        stat = self.stat
        self.stats[h].wait_recv()
        stat[h, 2] = stat[h, 0] + stat[h, 1]
        self.stats[h] = self.links.send(stat.at[h, 2], stat.at[h, 3], {"q": 1 - self.q})

    def stats_done(self, h, number):
        stat = self.stat
        self.stats[h].wait_recv()
        stats = (stat[h, 2] + stat[h, 3]) / self.width
        for i in range(number):
            self.cols[i, self.at(h)] = to_column(stats, i)

    def spread(self, h, blocks):
        here = self.out.at[0, self.at(h), self.mine]
        for k in blocks:
            if k:
                target = self.out.at[k, self.at(h), self.mine]
                self.spread_a[h, k] = self.links.send(here, target, {"a": across(self.a, k)})
        self.spread_p[h, 0] = self.links.send(here, here, {"p": 1 - self.p})

    def relay_p(self, h, k):
        if not k:
            return
        self.spread_a[h, k].wait_recv()
        here = self.out.at[k, self.at(h), self.mine]
        self.spread_p[h, k] = self.links.send(here, here, {"p": 1 - self.p})

    def relay_q(self, h, k):
        self.spread_p[h, k].wait_recv()
        here = self.out.at[k, self.at(h), self.pair]
        self.spread_q[h, k] = self.links.send(here, here, {"q": 1 - self.q})

    def arrived(self, h, k):
        self.spread_q[h, k].wait_recv()

    def steps(self, first, second, number, chain=False):
        def normed(h):
            self.stats_done(h, number)
            self.each(h, second)

        def spread_own(h):
            here = self.out.at[0, self.at(h), self.mine]
            self.spread_p[h, 0] = self.links.send(here, here, {"p": 1 - self.p})

        def spread_far(h, k):
            here = self.out.at[0, self.at(h), self.mine]
            target = self.out.at[k, self.at(h), self.mine]
            self.spread_a[h, k] = self.links.send(here, target, {"a": across(self.a, k)})

        table = {
            "P": self.send_p,
            "A": self.send_a,
            "SC": lambda h: self.scattered(h, first, number),
            "SQ": self.stats_q,
            "SD": normed,
            "X": spread_own,
            "Z": spread_far,
            "RP": self.relay_p,
            "RQ": self.relay_q,
        }
        if chain:
            lines = [
                Line(
                    self.links,
                    self.na,
                    lambda k, h=h: self.out.at[k, self.at(h), self.mine],
                    self.out.at[0, self.at(h), self.mine],
                )
                for h in range(HALVES)
            ]

            def pair_arrived(h, k):
                self.spread_p[h, k] = lines[h].to_pair(k)
                self.relay_q(h, k)

            table.update(
                X=lambda h: lines[h].to_pair(0).start(),
                Z=lambda h: lines[h].start(),
                FL=lambda h, t: lines[h].pass_on(1, t),
                FR=lambda h, t: lines[h].pass_on(-1, t),
                RQ=pair_arrived,
            )
        return table


class OverHeads:
    def __init__(self, links, na, a, p, q, held, from_a, out_ref):
        self.links, self.na, self.a, self.p, self.q = links, na, a, p, q
        self.held, self.from_a, self.out_ref = held, from_a, out_ref

    def to_pair(self):
        self.copy = self.links.send(self.held.at[0], self.held.at[1], {"p": 1 - self.p})

    def to_core(self):
        held = self.held
        self.copy.wait_recv()
        held[2] = held[0] + held[1]
        self.copy = self.links.send(held.at[2], held.at[3], {"q": 1 - self.q})

    def to_all(self):
        held = self.held
        self.copy.wait_recv()
        held[4] = held[2] + held[3]
        self.copies = [
            self.links.send(held.at[4], self.from_a.at[k - 1], {"a": across(self.a, k)})
            for k in range(1, self.na)
        ]

    def done(self):
        for copy in self.copies:
            copy.wait_recv()
        for k in range(self.na):
            for i in range(2):
                at = 2 * k + i
                total = self.held[4, at : at + 1]
                for j in range(1, self.na):
                    other = 2 * (k ^ j) + i
                    total = total + self.from_a[j - 1, other : other + 1]
                self.out_ref[at : at + 1] = total


def reduce_peers(na):
    a, p, q = lax.axis_index("a"), lax.axis_index("p"), lax.axis_index("q")
    return [{"q": 1 - q}, {"p": 1 - p}] + [{"a": across(a, k)} for k in range(1, na)]


def attn_math(r, tok_ref, gain_ref, proj_ref, inv_ref, res_ref):
    def first(at):
        own = r.add_all(at)
        proj_ref[at] = own
        r.parts[0, at] = fold(own * own)

    def second(at):
        own = proj_ref[at]
        inv = lax.rsqrt(r.cols[0, at] + epsilon)
        inv_ref[at] = inv
        residual = tok_ref[at].astype(f32) + own * wide(inv, r.quarter) * gain_ref[0:1]
        res_ref[at] = residual
        r.out[0, at, r.mine] = residual.astype(bf16)

    return first, second


def mlp_math(r, res_ref, grad_ref, gain_ref, block_ref, sum_ref):
    def first(at):
        own = r.add_all(at)
        r.total[at] = own
        r.parts[0, at] = fold(own * own)
        r.parts[1, at] = fold(grad_ref[at] * gain_ref[1:2] * own)

    def second(at):
        own = r.total[at]
        inv = wide(lax.rsqrt(r.cols[0, at] + epsilon), r.quarter)
        upstream = grad_ref[at]
        scaled = upstream * gain_ref[1:2]
        normed = own * inv
        block_ref[0, at, r.mine] = (res_ref[at] + normed * gain_ref[1:2]).astype(bf16)
        gains = upstream * normed
        sum_ref[...] += jnp.sum(gains.reshape(TILE // 8, 8, r.quarter), axis=0)
        grad = inv * scaled - own * inv * inv * inv * wide(r.cols[1, at], r.quarter)
        r.out[0, at, r.mine] = grad.astype(bf16)

    return first, second


def back_math(r, grad_ref, proj_ref, inv_ref, gain_ref, res_ref, sum_ref):
    def first(at):
        grad = grad_ref[at] + r.add_all(at)
        res_ref[at] = grad
        r.parts[0, at] = fold(grad * gain_ref[0:1] * proj_ref[at])

    def second(at):
        own = proj_ref[at]
        inv = wide(inv_ref[at], r.quarter)
        upstream = res_ref[at]
        gains = upstream * own * inv
        sum_ref[...] += jnp.sum(gains.reshape(TILE // 8, 8, r.quarter), axis=0)
        grad = inv * (upstream * gain_ref[0:1])
        grad = grad - own * inv * inv * inv * wide(r.cols[0, at], r.quarter)
        r.out[0, at, r.mine] = grad.astype(bf16)

    return first, second


MIDDLE = (
    ("F", 2), ("rP", 0, 2), ("F", 3), ("rP", 0, 3), ("rA", 0, 2), ("rP", 1, 3), ("rP", 1, 2), ("F", 1),
    ("rA", 0, 3), ("F", 0), ("rP", 0, 1), ("rA", 1, 3), ("rP", 1, 1), ("rP", 0, 0), ("rA", 1, 2),
    ("rP", 1, 0), ("rA", 0, 1), ("rA", 1, 1), ("rSC", 0), ("rSQ", 0), ("rSC", 1), ("rSD", 0), ("rZ", 0, 3),
    ("rX", 0), ("rSQ", 1), ("rSD", 1), ("rZ", 0, 1), ("BP",), ("rZ", 1, 3), ("rZ", 0, 2), ("rZ", 1, 1),
    ("rRP", 0, 3), ("rX", 1), ("rRP", 0, 1), ("rZ", 1, 2), ("rRQ", 0, 3), ("B", 0, 3), ("rRP", 0, 2),
    ("rRP", 1, 3), ("sP", 0, 3), ("rRQ", 0, 1), ("rRP", 1, 2), ("rRQ", 0, 2), ("rRQ", 1, 3), ("rRP", 1, 1),
    ("B", 0, 2), ("B", 0, 1), ("rRQ", 0, 0), ("sP", 0, 2), ("B", 1, 3), ("sP", 0, 1), ("rRQ", 1, 2),
    ("sA", 0, 3), ("B", 0, 0), ("sP", 1, 3), ("rRQ", 1, 1), ("sA", 0, 2), ("rRQ", 1, 0), ("B", 1, 2),
    ("sP", 0, 0), ("sA", 0, 1), ("B", 1, 1), ("sP", 1, 2), ("B", 1, 0), ("sA", 1, 3), ("sP", 1, 1),
    ("sSC", 0), ("sA", 1, 2), ("BQ",), ("sP", 1, 0), ("sSQ", 0), ("sA", 1, 1), ("sSD", 0), ("sZ", 0, 2),
    ("D",), ("sX", 0), ("sZ", 0, 1), ("sSC", 1), ("sSQ", 1), ("sZ", 0, 3), ("sRP", 0, 2), ("sSD", 1),
    ("sZ", 1, 1), ("sRP", 0, 1), ("sX", 1), ("sRQ", 0, 0), ("G", 2), ("sZ", 1, 3), ("G", 3), ("G", 1),
    ("sRP", 0, 3), ("G", 0), ("sZ", 1, 2), ("sRP", 1, 3), ("sRQ", 0, 1), ("sRQ", 1, 0), ("sRP", 1, 1),
    ("sRP", 1, 2), ("sRQ", 0, 2), ("sRQ", 0, 3), ("sRQ", 1, 3), ("sRQ", 1, 1), ("DS",), ("sRQ", 1, 2),
)


def middle_kernel(na, nb, *refs):
    x_ref, w_ref, res_ref, grad_ref, proj_ref, inv_ref, gain_ref = refs[:7]
    block_ref, back_out, ffn_sum_ref, grad_res_ref, attn_sum_ref, down_sum_ref, gu_grad_ref = refs[7:14]
    out, hidden_ref, grad_gu_ref, gu_ref, part_ref, down_grad, down_held = refs[14:21]
    scratch, (send_sem, recv_sem) = refs[21:-2], refs[-2:]
    units = hidden_ref.shape[2]
    width = x_ref.shape[2]
    b = lax.axis_index("b")
    greet(reduce_peers(na) + [{"b": across(b, j)} for j in range(1, nb)])
    links = Links(send_sem, recv_sem)
    r = Reduce(na, links, part_ref, out, scratch[:9])
    s = Reduce(na, links, part_ref, back_out, scratch[9:])
    ffn_sum_ref[...] = jnp.zeros_like(ffn_sum_ref)
    attn_sum_ref[...] = jnp.zeros_like(attn_sum_ref)
    wide_tile = 512

    def forward(k):
        def gated(n, carry):
            at, up_at = span(n, 256), pl.ds(pl.multiple_of(units + n * 256, 256), 256)
            gate = dot(x_ref[k], w_ref[:, at])
            up = dot(x_ref[k], w_ref[:, up_at])
            gu_ref[k, :, at] = gate
            gu_ref[k, :, up_at] = up
            hidden_ref[k, :, at] = (gate * jax.nn.sigmoid(gate) * up).astype(bf16)
            return carry

        lax.fori_loop(0, units // 256, gated, 0)

        def down(n, carry):
            at = span(n, wide_tile)
            part_ref[k, :, at] = dot_t(hidden_ref[k], w_ref[at, 2 * units :]).astype(bf16)
            return carry

        lax.fori_loop(0, width // wide_tile, down, 0)

    def backward(h, k):
        rows = r.at(h)

        def gated(n, carry):
            at, up_at = span(n, 256), pl.ds(pl.multiple_of(units + n * 256, 256), 256)
            down_at = pl.ds(pl.multiple_of(2 * units + n * 256, 256), 256)
            grad_hidden = dot(out[k, rows], w_ref[:, down_at])
            gate, up = gu_ref[k, rows, at], gu_ref[k, rows, up_at]
            sigmoid = jax.nn.sigmoid(gate)
            active = gate * sigmoid
            grad_gu_ref[k, rows, at] = (
                grad_hidden * up * (sigmoid * (1.0 + gate * (1.0 - sigmoid)))
            ).astype(bf16)
            grad_gu_ref[k, rows, up_at] = (grad_hidden * active).astype(bf16)
            return carry

        lax.fori_loop(0, units // 256, gated, 0)

        def back(n, carry):
            at = span(n, wide_tile)
            part_ref[k, rows, at] = dot_t(
                grad_gu_ref[k, rows], w_ref[at, : 2 * units]
            ).astype(bf16)
            return carry

        lax.fori_loop(0, width // wide_tile, back, 0)

    first, second = mlp_math(r, res_ref, grad_ref, gain_ref, block_ref, ffn_sum_ref)
    back_first, back_second = back_math(
        s, grad_ref, proj_ref, inv_ref, gain_ref, grad_res_ref, attn_sum_ref
    )
    copies, reused = {}, []
    columns = slice(0, units)

    def forward_step(k):
        forward(k)
        for h in range(HALVES):
            r.send_q(h, k)

    def backward_step(h, k):
        if not reused:
            links.sent(r.step_q.values())
            reused.append(True)
        r.arrived(h, k)
        backward(h, k)
        s.send_q(h, k)

    def block_p():
        here = block_ref.at[0, :, r.mine]
        copies["p"] = links.send(here, here, {"p": 1 - r.p})

    def block_q():
        copies["p"].wait_recv()
        here = block_ref.at[0, :, r.pair]
        copies["q"] = links.send(here, here, {"q": 1 - r.q})

    def down_grads():
        for block in range(na):
            weight_grad(out, hidden_ref, down_grad, block)
        copies["b"] = exchange_b(links, down_grad, down_held, columns)

    table = {
        "F": forward_step,
        "B": backward_step,
        "BP": block_p,
        "BQ": block_q,
        "D": down_grads,
        "DS": lambda: sum_b(
            copies["b"], lambda block: down_grad.at[block, b], down_held, down_sum_ref, columns
        ),
        "G": lambda block: weight_grad(x_ref, grad_gu_ref, gu_grad_ref, block),
    }
    table.update({"r" + key: step for key, step in r.steps(first, second, 2).items()})
    table.update({"s" + key: step for key, step in s.steps(back_first, back_second, 1).items()})
    for key, *where in MIDDLE:
        table[key](*where)
    for h in range(HALVES):
        for k in range(na):
            s.arrived(h, k)
    copies["q"].wait_recv()
    links.finish()


def middle_call(nb, x_all, w_mlp, res_mine, grad_mine, proj_mine, inv_mine, width_gain):
    na, rows, width = x_all.shape
    quarter, units = width // 4, w_mlp.shape[1] // 3
    w_rows = width // (na * nb)
    vmem = pl.BlockSpec(memory_space=pltpu.VMEM)
    shape = jax.ShapeDtypeStruct
    outs = (
        shape((1, rows, width), bf16),
        shape((na, rows, width), bf16),
        shape((8, quarter), f32),
        shape((rows, quarter), f32),
        shape((8, quarter), f32),
        shape((na, w_rows, units), bf16),
        shape((na, nb, w_rows, 2 * units), bf16),
    )
    copies = 2 * HALVES * (6 * na + 1) + 2 + nb
    return pl.pallas_call(
        functools.partial(middle_kernel, na, nb),
        out_shape=outs,
        in_specs=[vmem] * 7,
        out_specs=(vmem,) * len(outs),
        scratch_shapes=[
            pltpu.VMEM((na, rows, width), bf16),
            pltpu.VMEM((na, rows, units), bf16),
            pltpu.VMEM((na, rows, 2 * units), bf16),
            pltpu.VMEM((na, rows, 2 * units), f32),
            pltpu.VMEM((na, rows, width), bf16),
            pltpu.VMEM((na, nb, w_rows, units), bf16),
            pltpu.VMEM((nb - 1, na, w_rows, units), bf16),
        ]
        + reduce_scratch(na, rows, width)
        + reduce_scratch(na, rows, width)
        + [pltpu.SemaphoreType.DMA((copies,)), pltpu.SemaphoreType.DMA((copies,))],
        compiler_params=pltpu.CompilerParams(
            collective_id=2, has_side_effects=True, vmem_limit_bytes=VMEM_LIMIT
        ),
        name="middle",
    )(x_all, w_mlp, res_mine, grad_mine, proj_mine, inv_mine, width_gain)


def last_kernel(na, nb, *refs):
    proj_ref, x_far, qkv_ref, stats_ref, gain_ref, cos_ref, sin_ref, w_ref, att_ref = refs[:9]
    grad_ref, attn_sum_ref, ffn_sum_ref, down_sum_ref, gu_grad_far = refs[9:14]
    out, sums_ref, down_far, gu_far, qkv_out, wout_out = refs[14:20]
    scaled_ref, grad_qkv_ref, part_ref, head_sums, held, stats_a, inner_ref = refs[20:27]
    own_sums, a_sums, b_sums, gu_held, gu_sum, attn_grad, attn_held, attn_sum = refs[27:35]
    down_in, gu_in, attn_in, x_ref, gu_own, down_out, gu_out = refs[35:42]
    scratch, (local_sem, send_sem, recv_sem) = refs[42:-3], refs[-3:]
    links = Links(send_sem, recv_sem)
    load_gu = pltpu.make_async_copy(
        gu_grad_far.at[:, lax.axis_index("b")], gu_own, local_sem.at[0]
    )
    load_gu.start()
    load_x = pltpu.make_async_copy(x_far, x_ref, local_sem.at[1])
    load_x.start()
    r = Reduce(na, links, part_ref, out, scratch)
    a, b, p, q, mine, pair, quarter = (
        r.a, lax.axis_index("b"), r.p, r.q, r.mine, r.pair, r.quarter,
    )
    units = down_sum_ref.shape[2]
    own_sums[...] = jnp.zeros_like(own_sums)
    own_sums[0:1, mine] = jnp.sum(attn_sum_ref[...], axis=0, keepdims=True)
    own_sums[1:2, mine] = jnp.sum(ffn_sum_ref[...], axis=0, keepdims=True)
    greet(reduce_peers(na) + [{"b": across(b, j)} for j in range(1, nb)])
    far = list(range(2, na)) + [1]

    def to_owners(source, target, columns):
        return [
            (k, links.send(
                source.at[across(a, k), :, columns], target.at[k - 1, :, columns], {"a": across(a, k)}
            ))
            for k in far
        ]

    whole = slice(0, units)
    halves = [slice(0, units), slice(units, 2 * units)]
    down_copies = to_owners(down_sum_ref, down_in, whole)
    gu_b = [exchange_b(links, gu_grad_far, gu_held, columns) for columns in halves]
    here = own_sums.at[:, mine]
    sums_p = links.send(here, here, {"p": 1 - p})

    held[0] = jnp.zeros_like(held[0])
    head_sums[...] = jnp.zeros_like(head_sums)

    def attend_back(k, carry):
        queries, key_rows, values, q_inv, k_inv, q_rot, k_rot, probs = attention(
            k, qkv_ref[k], stats_ref[...], gain_ref, cos_ref, sin_ref
        )
        cos_table, sine_table = cos_ref[...], sin_ref[...]
        grad_att = dot(proj_ref[k], w_ref[:, 3 * HD :]).astype(bf16)
        grad_v = t_dot(probs.astype(bf16), grad_att)
        grad_p = dot_t(grad_att, values)
        delta = jnp.sum(probs * grad_p, axis=1, keepdims=True)
        grad_scores = (probs * (grad_p - delta) * HD ** (-0.5)).astype(bf16)
        grad_q = dot(grad_scores, k_rot)
        grad_k = t_dot(grad_scores, q_rot)
        grad_q = grad_q * cos_table + rotate_back(grad_q * sine_table)
        grad_k = grad_k * cos_table + rotate_back(grad_k * sine_table)
        head_sums[0:1] += jnp.sum(grad_q * queries * q_inv, axis=0, keepdims=True)
        head_sums[1:2] += jnp.sum(grad_k * key_rows * k_inv, axis=0, keepdims=True)
        scaled_q = grad_q * gain_ref[0:1]
        scaled_k = grad_k * gain_ref[1:2]
        scaled_ref[k, :, :HD] = scaled_q
        scaled_ref[k, :, HD:] = scaled_k
        grad_qkv_ref[k, :, 2 * HD :] = grad_v.astype(bf16)
        held[0] += to_row(scaled_q * queries, 2 * k) + to_row(scaled_k * key_rows, 2 * k + 1)
        return carry

    lax.fori_loop(0, na, attend_back, 0)
    sums_p.wait_recv()
    here = own_sums.at[:, pair]
    sums_q = links.send(here, here, {"q": 1 - q})
    gu_copies = []

    def sent():
        for block in range(na):
            weight_grad(proj_ref, att_ref, attn_grad, block, slice(3 * HD, 4 * HD))
        load_gu.wait()
        sum_b(gu_b[0], lambda block: gu_own.at[block], gu_held, gu_sum, halves[0])
        gu_copies.append(to_owners(gu_sum, gu_in, halves[0]))

    over_heads = OverHeads(links, na, a, p, q, held, stats_a, inner_ref)
    over_heads.to_pair()
    over_heads.to_core()
    over_heads.to_all()
    sent()
    over_heads.done()

    def qkv_back(k):
        for i in range(2):
            at = slice(i * HD, (i + 1) * HD)
            inv = lax.rsqrt(to_column(stats_ref[...] / HQ, 2 * k + i) + epsilon)
            mean = to_column(inner_ref[...] / HQ, 2 * k + i)
            grad = inv * scaled_ref[k, :, at] - qkv_ref[k, :, at] * inv * inv * inv * mean
            grad_qkv_ref[k, :, at] = grad.astype(bf16)

        def part(n, carry):
            at = span(n, 512)
            part_ref[k, :, at] = dot_t(grad_qkv_ref[k], w_ref[at, : 3 * HD]).astype(bf16)
            return carry

        lax.fori_loop(0, part_ref.shape[2] // 512, part, 0)

    for k in r.lead:
        qkv_back(k)
        for h in range(HALVES):
            r.send_q(h, k)
    for h in range(HALVES):
        for k in r.lead:
            r.send_p(h, k)
    load_x.wait()
    for block in range(na):
        weight_grad(x_ref, grad_qkv_ref, attn_grad, block, slice(0, 3 * HD))
    attn_columns = slice(0, 4 * HD)
    attn_b = exchange_b(links, attn_grad, attn_held, attn_columns)
    for h in range(HALVES):
        for k in r.lead:
            r.send_a(h, k)
    sums_q.wait_recv()
    sums_a = [
        links.send(own_sums.at[:, span(across(a, k), quarter)], a_sums.at[k - 1], {"a": across(a, k)})
        for k in range(1, na)
    ]
    sum_b(gu_b[1], lambda block: gu_own.at[block], gu_held, gu_sum, halves[1])
    gu_copies.append(to_owners(gu_sum, gu_in, halves[1]))

    def first(at):
        out[0, at, mine] = (grad_ref[at] + r.add_all(at)).astype(bf16)

    for h in range(HALVES):
        r.scattered(h, first, 0)
        r.spread(h, [0])
    for copy in sums_a:
        copy.wait_recv()
    total = own_sums[:, span(a, quarter)]
    for k in range(1, na):
        total = total + a_sums[k - 1]
    b_sums[0, :, :quarter] = total
    b_sums[0, :, quarter:] = head_sums[...]
    sums_b = [links.send(b_sums.at[0], b_sums.at[j], {"b": across(b, j)}) for j in range(1, nb)]
    for h in range(HALVES):
        r.relay_q(h, 0)
    sum_b(attn_b, lambda block: attn_grad.at[block, b], attn_held, attn_sum, attn_columns)
    attn_copies = to_owners(attn_sum, attn_in, attn_columns)

    def store(target, index, size, value):
        target[:, span(index, size)] = value.astype(f32)

    store(down_out, a, units, down_sum_ref[a])
    for c in range(2):
        gu_out[:, c, span(a, units)] = gu_sum[a, :, halves[c]].astype(f32)
    for c in range(3):
        store(qkv_out.at[c], a, HD, attn_sum[a, :, c * HD : (c + 1) * HD])
    store(wout_out, a, HD, attn_sum[a, :, 3 * HD :])
    for k, copy in down_copies:
        copy.wait_recv()
        store(down_out, across(a, k), units, down_in[k - 1])
    save_down = pltpu.make_async_copy(down_out, down_far, local_sem.at[2])
    save_down.start()
    for copy in sums_b:
        copy.wait_recv()
    total = b_sums[0]
    for j in range(1, nb):
        total = total + b_sums[j]
    sums_ref[...] = total
    for c in range(2):
        for k, copy in gu_copies[c]:
            copy.wait_recv()
            gu_out[:, c, span(across(a, k), units)] = gu_in[k - 1, :, halves[c]].astype(f32)
    save_gu = pltpu.make_async_copy(gu_out, gu_far, local_sem.at[3])
    save_gu.start()
    for k, copy in attn_copies:
        copy.wait_recv()
        for c in range(3):
            store(qkv_out.at[c], across(a, k), HD, attn_in[k - 1, :, c * HD : (c + 1) * HD])
        store(wout_out, across(a, k), HD, attn_in[k - 1, :, 3 * HD :])
    for h in range(HALVES):
        r.arrived(h, 0)
    save_down.wait()
    save_gu.wait()
    links.finish()


def last_call(nb, *operands):
    na, rows, width = operands[0].shape
    w_rows, units = operands[12].shape[1:]
    quarter = width // 4
    vmem, far = pl.BlockSpec(memory_space=pltpu.VMEM), pl.BlockSpec(memory_space=pl.ANY)
    shape = jax.ShapeDtypeStruct
    outs = (
        shape((1, rows, width), bf16),
        shape((8, quarter + HD), f32),
        shape((w_rows, na * units), f32),
        shape((w_rows, 2, na * units), f32),
        shape((3, w_rows, na * HD), f32),
        shape((w_rows, na * HD), f32),
    )
    copies = HALVES * (3 * na + 1) + 2 + 6 * na + 4 * nb
    return pl.pallas_call(
        functools.partial(last_kernel, na, nb),
        out_shape=outs,
        in_specs=[far if i in (1, 13) else vmem for i in range(14)],
        out_specs=(vmem, vmem, far, far, vmem, vmem),
        scratch_shapes=[
            pltpu.VMEM((na, rows, 2 * HD), f32),
            pltpu.VMEM((na, rows, 3 * HD), bf16),
            pltpu.VMEM((na, rows, width), bf16),
            pltpu.VMEM((8, HD), f32),
            pltpu.VMEM((5, 8, rows), f32),
            pltpu.VMEM((na - 1, 8, rows), f32),
            pltpu.VMEM((8, rows), f32),
            pltpu.VMEM((8, width), f32),
            pltpu.VMEM((na - 1, 8, quarter), f32),
            pltpu.VMEM((nb, 8, quarter + HD), f32),
            pltpu.VMEM((nb - 1, na, w_rows, 2 * units), bf16),
            pltpu.VMEM((na, w_rows, 2 * units), bf16),
            pltpu.VMEM((na, nb, w_rows, 4 * HD), bf16),
            pltpu.VMEM((nb - 1, na, w_rows, 4 * HD), bf16),
            pltpu.VMEM((na, w_rows, 4 * HD), bf16),
            pltpu.VMEM((na - 1, w_rows, units), bf16),
            pltpu.VMEM((na - 1, w_rows, 2 * units), bf16),
            pltpu.VMEM((na - 1, w_rows, 4 * HD), bf16),
            pltpu.VMEM((na, rows, width), bf16),
            pltpu.VMEM((na, w_rows, 2 * units), bf16),
            pltpu.VMEM((w_rows, na * units), f32),
            pltpu.VMEM((w_rows, 2, na * units), f32),
        ]
        + reduce_scratch(na, rows, width)
        + [
            pltpu.SemaphoreType.DMA((4,)),
            pltpu.SemaphoreType.DMA((copies,)),
            pltpu.SemaphoreType.DMA((copies,)),
        ],
        compiler_params=pltpu.CompilerParams(
            collective_id=4, has_side_effects=True, vmem_limit_bytes=VMEM_LIMIT
        ),
        name="last",
    )(*operands)


def reduce_scratch(na, rows, width):
    quarter = width // 4
    return [
        pltpu.VMEM((na, rows, width // 2), bf16),
        pltpu.VMEM((na, rows, width // 2), bf16),
        pltpu.VMEM((na, rows, quarter), bf16),
        pltpu.VMEM((na - 1, rows, quarter), bf16),
        pltpu.VMEM((na - 1, rows, quarter), bf16),
        pltpu.VMEM((rows, quarter), f32),
        pltpu.VMEM((2, rows, 128), f32),
        pltpu.VMEM((2, rows, 128), f32),
        pltpu.VMEM((HALVES, 4, 8, rows // HALVES), f32),
    ]


ENTER = (
    ("Z", 0), ("W", 3), ("FW", 0), ("FR", 0, 1), ("FL", 0, 1), ("W", 1), ("CUT", 2), ("FW", 1), ("W", 2),
    ("FR", 0, 2), ("FR", 0, 3), ("CUT", 3), ("M", 0, 3), ("FL", 0, 2), ("CUT", 1), ("FW", 3), ("FL", 0, 3),
    ("GA",), ("FT", 0), ("FQ", 3), ("FW", 2), ("CUT", 0), ("FQ", 2), ("M", 0, 1), ("M", 2, 3), ("FQ", 1),
    ("J", 3), ("FQ", 0), ("J", 0), ("GB",), ("M", 1, 1), ("J", 1), ("J", 2), ("S1",), ("S2",), ("S3",),
    ("M", 1, 3), ("MR", 1, 0), ("M", 1, 2), ("S4",), ("E", 3), ("E", 1), ("rP", 1, 3), ("E", 2),
    ("rP", 1, 1), ("M", 2, 1), ("MR", 2, 3), ("rP", 0, 3), ("rP", 0, 1), ("MR", 0, 3), ("E", 0),
    ("rA", 1, 3), ("MR", 2, 0), ("rA", 1, 1), ("MR", 0, 1), ("rA", 0, 3), ("MR", 1, 3), ("rP", 0, 2),
    ("MR", 2, 1), ("rA", 0, 2), ("rA", 0, 1), ("rP", 0, 0), ("rP", 1, 2), ("rA", 1, 2), ("MR", 1, 2),
    ("rP", 1, 0), ("rSC", 0), ("rSQ", 0), ("MR", 0, 0), ("M", 2, 2), ("rSC", 1), ("rSD", 0), ("rSQ", 1),
    ("rX", 0), ("rSD", 1), ("rZ", 0), ("rZ", 1), ("rFR", 0, 1), ("rFL", 0, 1), ("rX", 1), ("MR", 2, 2),
    ("rFR", 1, 1), ("rFL", 1, 1), ("rFR", 0, 2), ("rRQ", 0, 0), ("rFL", 1, 2), ("rFL", 0, 2), ("MR", 1, 1),
    ("rFR", 0, 3), ("M", 0, 2), ("rFR", 1, 2), ("rFL", 1, 3), ("rFR", 1, 3), ("rFL", 0, 3), ("rRQ", 0, 1),
    ("MR", 0, 2), ("rRQ", 1, 1), ("rRQ", 1, 2), ("rRQ", 0, 2), ("rRQ", 1, 0), ("rRQ", 1, 3), ("rRQ", 0, 3),
)


def enter_kernel(na, nb, *refs):
    tok_ref, qkv_w_ref, wout_ref, gu_ref, down_ref, cos_ref, sin_ref = refs[:7]
    gain_refs = refs[7:11]
    x_far, w_far, mlp_w_ref, width_gain_ref, head_gain_ref, qkv_far, stats_ref, att_far = refs[11:19]
    out, proj_ref, inv_ref, res_ref = refs[19:23]
    own_gains, gains_ref, piece_ref, part_ref, held, stats_a = refs[23:29]
    x_ref, w_ref, qkv_ref, att_ref = refs[29:33]
    scratch, (local_sem, send_sem, recv_sem) = refs[33:-3], refs[-3:]
    saves = [
        pltpu.make_async_copy(near, there, local_sem.at[5 + i])
        for i, (near, there) in enumerate(
            ((x_ref, x_far), (w_ref, w_far), (qkv_ref, qkv_far), (att_ref, att_far))
        )
    ]
    a, b, p, q = (lax.axis_index(axis) for axis in ("a", "b", "p", "q"))
    rows = wout_ref.shape[0]
    quarter = tok_ref.shape[1]
    units = down_ref.shape[1] // na
    own_gains[...] = jnp.zeros_like(own_gains)
    for i, ref in enumerate(gain_refs):
        own_gains[i : i + 1, : ref.shape[1]] = ref[...].astype(f32)
    gains_ref[a, b] = own_gains[...]
    greet(
        [{"q": 1 - q}, {"p": 1 - p}]
        + [{"a": across(a, k)} for k in range(1, na)]
        + [{"b": across(b, j)} for j in range(1, nb)]
    )
    links = Links(send_sem, recv_sem)
    mine, pair = span(2 * q + p, quarter), span(q, 2 * quarter)
    place = span(a * nb + b, rows)
    copies, ends = {}, []
    locals_ = [pltpu.make_async_copy(tok_ref, x_ref.at[0, :, mine], local_sem.at[0])]

    def weight_sources(k):
        block = span(across(a, k), HD)
        sources = [qkv_w_ref.at[c, :, block] for c in range(3)] + [wout_ref.at[:, block]]
        return [(s, w_ref.at[place, c * HD : (c + 1) * HD]) for c, s in enumerate(sources)]

    for c, (source, target) in enumerate(weight_sources(0)):
        locals_.append(pltpu.make_async_copy(source, target, local_sem.at[1 + c]))
    for copy in locals_:
        copy.start()

    def send_gains():
        copies["g"] = [
            links.send(own_gains, gains_ref.at[a, b], {"a": across(a, k)}) for k in range(1, na)
        ]

    def relay_gains():
        for copy in copies["g"]:
            copy.wait_recv()
        at = gains_ref.at[:, b]
        copies["gb"] = [links.send(at, at, {"b": across(b, j)}) for j in range(1, nb)]

    def send_weights(k):
        copies["w", k] = [
            links.send(source, target, {"a": across(a, k)}) for source, target in weight_sources(k)
        ]

    def relay_weights(k):
        if k:
            for copy in copies["w", k]:
                copy.wait_recv()
        else:
            for copy in locals_[1:]:
                copy.wait()
        at = w_ref.at[span(across(a, k) * nb + b, rows), :]
        copies["wb", k] = [links.send(at, at, {"b": across(b, j)}) for j in range(1, nb)]

    line = Line(links, na, lambda k: x_ref.at[k, :, mine], tok_ref)

    def own_tokens(_):
        locals_[0].wait()
        line.to_pair(0).start()

    def pair_tokens(k):
        line.to_pair(k).wait_recv()
        at = x_ref.at[k, :, pair]
        copies["x", k] = links.send(at, at, {"q": 1 - q})

    def cut_weights(k):
        block = span(across(a, k), units)

        def cut(i, carry):
            at = pl.ds(pl.multiple_of(i * TILE, TILE), TILE)
            cuts = (gu_ref[at, 0, block], gu_ref[at, 1, block], down_ref[at, block])
            for c in range(3):
                if k:
                    piece_ref[k - 1, c, at] = cuts[c]
                else:
                    to = pl.ds(pl.multiple_of((a * nb + b) * rows + i * TILE, TILE), TILE)
                    mlp_w_ref[to, c * units : (c + 1) * units] = cuts[c]
            return carry

        lax.fori_loop(0, rows // TILE, cut, 0)

    def send_piece(c, k):
        target = mlp_w_ref.at[place, c * units : (c + 1) * units]
        copies["m", c, k] = links.send(piece_ref.at[k - 1, c], target, {"a": across(a, k)})

    def relay_piece(c, k):
        if k:
            copies["m", c, k].wait_recv()
        at = mlp_w_ref.at[span(across(a, k) * nb + b, rows), c * units : (c + 1) * units]
        ends.extend(links.send(at, at, {"b": across(b, j)}) for j in range(1, nb))

    arrived, ready = set(), []

    def project(k):
        if not arrived:
            held[0] = jnp.zeros_like(held[0])
            for i in range(na):
                for copy in copies["wb", i]:
                    copy.wait_recv()
        arrived.add(k)
        copies["x", k].wait_recv()

        def chunk(i, carry):
            at = span(i, 128)
            proj = dot(x_ref[k, at], w_ref[:, : 3 * HD])
            qkv_ref[k, at] = proj
            queries, key_rows = proj[:, :HD], proj[:, HD : 2 * HD]
            held[0, :, at] += to_row(queries * queries, 2 * k) + to_row(key_rows * key_rows, 2 * k + 1)
            return carry

        lax.fori_loop(0, x_ref.shape[1] // 128, chunk, 0)

    over_heads = OverHeads(links, na, a, p, q, held, stats_a, stats_ref)

    def all_stats():
        for save in saves[:3]:
            save.start()
        over_heads.done()
        for copy in copies["gb"]:
            copy.wait_recv()
        n_d, n_h = gain_refs[0].shape[1], gain_refs[2].shape[1]
        width_gain_ref[...] = jnp.zeros_like(width_gain_ref)
        head_gain_ref[...] = jnp.zeros_like(head_gain_ref)
        for i in range(2):
            width_gain_ref[i : i + 1] = jnp.concatenate(
                [gains_ref[2 * q + p, j, i : i + 1, :n_d] for j in range(nb)], axis=1
            )
            head_gain_ref[i : i + 1] = jnp.concatenate(
                [gains_ref[a, j, i + 2 : i + 3, :n_h] for j in range(nb)], axis=1
            )

    r = Reduce(na, links, part_ref, out, scratch)

    def attend(k):
        values, probs = (
            attention(k, qkv_ref[k], stats_ref[...], head_gain_ref, cos_ref, sin_ref)[i] for i in (2, 7)
        )
        attended = dot(probs.astype(bf16), values).astype(bf16)
        att_ref[k] = attended

        def part(n, carry):
            at = span(n, 512)
            part_ref[k, :, at] = dot_t(att_ref[k], w_ref[at, 3 * HD :]).astype(bf16)
            return carry

        lax.fori_loop(0, part_ref.shape[2] // 512, part, 0)
        for h in range(HALVES):
            r.send_q(h, k)

    first, second = attn_math(r, tok_ref, width_gain_ref, proj_ref, inv_ref, res_ref)
    table = {
        "GA": send_gains,
        "GB": relay_gains,
        "W": send_weights,
        "FW": relay_weights,
        "Z": lambda _: line.start(),
        "FL": lambda _, t: line.pass_on(1, t),
        "FR": lambda _, t: line.pass_on(-1, t),
        "FT": own_tokens,
        "FQ": pair_tokens,
        "CUT": cut_weights,
        "M": send_piece,
        "MR": relay_piece,
        "J": project,
        "S1": over_heads.to_pair,
        "S2": over_heads.to_core,
        "S3": over_heads.to_all,
        "S4": all_stats,
        "E": attend,
    }
    table.update({"r" + key: step for key, step in r.steps(first, second, 1, True).items()})
    for key, *where in ENTER:
        table[key](*where)
    saves[3].start()
    for h in range(HALVES):
        for k in range(na):
            r.arrived(h, k)
    for copy in ends:
        copy.wait_recv()
    for save in saves:
        save.wait()
    links.finish()


def enter_call(na, nb, tok_mine, qkv, w_out, gu, down, cos_table, sine_table, gains):
    rows, quarter = tok_mine.shape
    width = 4 * quarter
    w_rows, units = down.shape[0], down.shape[1] // na
    lanes = max(128, gains[0].shape[1])
    vmem, far = pl.BlockSpec(memory_space=pltpu.VMEM), pl.BlockSpec(memory_space=pl.ANY)
    shape = jax.ShapeDtypeStruct
    full = shape((na, rows, width), bf16)
    outs = [
        full,
        shape((width, 4 * HD), bf16),
        shape((width, 3 * units), bf16),
        shape((8, quarter), f32),
        shape((8, HD), f32),
        shape((na, rows, 3 * HD), f32),
        shape((8, rows), f32),
        shape((na, rows, HD), bf16),
        full,
        shape((rows, quarter), f32),
        shape((rows, 128), f32),
        shape((rows, quarter), f32),
    ]
    copies = 90 + 16 * nb
    return pl.pallas_call(
        functools.partial(enter_kernel, na, nb),
        out_shape=tuple(outs),
        in_specs=[vmem] * 11,
        out_specs=tuple(far if i in (0, 1, 5, 7) else vmem for i in range(len(outs))),
        scratch_shapes=[
            pltpu.VMEM((8, lanes), f32),
            pltpu.VMEM((na, nb, 8, lanes), f32),
            pltpu.VMEM((na - 1, 3, w_rows, units), bf16),
            pltpu.VMEM((na, rows, width), bf16),
            pltpu.VMEM((5, 8, rows), f32),
            pltpu.VMEM((na - 1, 8, rows), f32),
            pltpu.VMEM((na, rows, width), bf16),
            pltpu.VMEM((width, 4 * HD), bf16),
            pltpu.VMEM((na, rows, 3 * HD), f32),
            pltpu.VMEM((na, rows, HD), bf16),
        ]
        + reduce_scratch(na, rows, width)
        + [
            pltpu.SemaphoreType.DMA((9,)),
            pltpu.SemaphoreType.DMA((copies,)),
            pltpu.SemaphoreType.DMA((copies,)),
        ],
        compiler_params=pltpu.CompilerParams(
            collective_id=5, has_side_effects=True, vmem_limit_bytes=VMEM_LIMIT
        ),
        name="enter",
    )(tok_mine, qkv, w_out, gu, down, cos_table, sine_table, *gains)


def rope_tables(length, width):
    half_width = width // 2
    inv_freq = rope_base ** (-(jnp.arange(half_width, dtype=f32) * 2.0) / width)
    angles = jnp.arange(length, dtype=f32)[:, None] * inv_freq[None, :]
    cos_table = jnp.concatenate([jnp.cos(angles), jnp.cos(angles)], axis=1)
    sine_table = jnp.concatenate([jnp.sin(angles), jnp.sin(angles)], axis=1)
    return cos_table, sine_table


def on_device(
    tokens,
    qkv_weight,
    out_weight,
    gu_weight,
    down_weight,
    attn_gain,
    ffn_gain,
    q_gain,
    k_gain,
    out_grad,
):
    na, nb = lax.axis_size("a"), lax.axis_size("b")
    a, b = lax.axis_index("a"), lax.axis_index("b")
    share = lax.axis_index("q") * 2 + lax.axis_index("p")
    rows, width = tokens.shape
    quarter = width // 4
    w_rows = out_weight.shape[0]
    units = down_weight.shape[1] // na

    def quarter_of(operand):
        return lax.dynamic_slice_in_dim(operand, share * quarter, quarter, 1)

    tok_mine, grad_mine = quarter_of(tokens), quarter_of(out_grad)
    cos_table, sine_table = rope_tables(SEQ_LEN, HD)
    (
        x_all,
        w_attn,
        w_mlp,
        width_gain,
        head_gain,
        qkv,
        stats,
        attended,
        res_all,
        proj_mine,
        inv_mine,
        res_mine,
    ) = enter_call(
        na,
        nb,
        tok_mine,
        qkv_weight.transpose(1, 0, 2),
        out_weight,
        gu_weight,
        down_weight,
        cos_table,
        sine_table,
        [gain[None] for gain in (attn_gain, ffn_gain, q_gain, k_gain)],
    )
    n_d, n_h = attn_gain.shape[0], q_gain.shape[0]
    block_rows, grad_proj, ffn_sums, grad_res, attn_sums, down_sum, gu_grad = middle_call(
        nb, res_all, w_mlp, res_mine, grad_mine, proj_mine, inv_mine, width_gain
    )
    grad_rows, sums, down_grad, gu_grad, qkv_grad, out_grad_w = last_call(
        nb,
        grad_proj,
        x_all,
        qkv,
        stats,
        head_gain,
        cos_table,
        sine_table,
        w_attn,
        attended,
        grad_res,
        attn_sums,
        ffn_sums,
        down_sum,
        gu_grad,
    )
    width_sums = lax.dynamic_slice_in_dim(sums[:2, :quarter], b * n_d, n_d, 1)
    head_sums = lax.dynamic_slice_in_dim(sums[:2, quarter:], b * n_h, n_h, 1)
    return (
        block_rows[0].astype(f32),
        grad_rows[0].astype(f32),
        qkv_grad.transpose(1, 0, 2),
        out_grad_w,
        gu_grad,
        down_grad,
        width_sums[0],
        width_sums[1],
        head_sums[0],
        head_sums[1],
    )


def solution(mesh):
    dp, tp = mesh.shape["dp"], mesh.shape["tensor"]
    na = HEADS // tp
    fine = Mesh(mesh.devices.reshape(na, dp // na, tp // 2, 2), ("a", "b", "p", "q"))
    dp_axes, tp_axes = ("a", "b"), ("p", "q")
    both = tp_axes + dp_axes
    return jax.shard_map(
        on_device,
        mesh=fine,
        in_specs=(
            P(dp_axes, None),
            P(dp_axes, None, tp_axes),
            P(dp_axes, tp_axes),
            P(dp_axes, None, tp_axes),
            P(dp_axes, tp_axes),
            P(dp_axes),
            P(dp_axes),
            P(both),
            P(both),
            P(dp_axes, None),
        ),
        out_specs=(
            P(dp_axes, None),
            P(dp_axes, None),
            P(dp_axes, None, tp_axes),
            P(dp_axes, tp_axes),
            P(dp_axes, None, tp_axes),
            P(dp_axes, tp_axes),
            P(dp_axes),
            P(dp_axes),
            P(both),
            P(both),
        ),
        check_vma=False,
    )
```

profile of v0, /device:TPU:8, one launch (start us, length us, event | category | flops | bytes accessed | tf_op | source)
XLA Modules:
  0.0 443.2 jit_solution(13614585741202191631)
XLA Ops:
  0.6 0.0 copy-start
  0.7 1.8 constant_dynamic-slice_fusion.3.refs_0_
  2.5 0.5 fusion
  3.0 0.8 pad_maximum_fusion
  3.8 1.2 broadcast_in_dim.14.refs_7_
  5.1 1.2 broadcast_in_dim.15.refs_8_
  6.3 155.9 %enter.1 = (bf16[4,256,2048]{2,1,0:T(8,128)(2,1)}, bf16[2048,512]{1,0:T(8,128)(2,1)}, bf16[2048,1536]{1,0:T(8,128)(2,1)}, f32[8,512]{1,0:T(8,128)}, f32[8,128]{1...) custom-call(bf16[256,512]{1,0:T(8,128)(2,1)} %constant_dynamic-slice, ...), custom_call_target="tpu_custom_call" | custom-call | tf_op jit(solution)/shard_map/enter/pallas_call | solution.py:1204
  162.2 0.8 constant_dynamic-slice_fusion.2.refs_3_
  163.0 137.4 %middle.1 = (bf16[1,256,2048]{2,1,0:T(8,128)(2,1)}, bf16[4,256,2048]{2,1,0:T(8,128)(2,1)}, f32[8,512]{1,0:T(8,128)}, f32[256,512]{1,0:T(8,128)}, f32[8,512]{1,0:...) custom-call(bf16[4,256,2048]{2,1,0:T(8,128)(2,1)} %get-tuple-element.35.refs_0_, ...), custom_call_target="tpu_custom_call" | custom-call | tf_op jit(solution)/shard_map/middle/pallas_call | solution.py:686
  300.5 128.4 %last.1 = (bf16[1,256,2048]{2,1,0:T(8,128)(2,1)}, f32[8,640]{1,0:T(8,128)}, f32[256,2048]{1,0:T(8,128)}, f32[256,2,2048]{2,1,0:T(2,128)}, f32[3,256,512]{2,1,0:T(8,128)}, /*index=5*/f32[256,512]{1,0:T(8,128)}) custom-call(bf16[4,256,2048]{2,1,0:T(8,128)(2,1)} %get-tuple-element.42.refs_0_, bf16[4,256,2048]{2,1,0:T(8,128)(2,1)} %get-tuple-element.43.refs_1_, ...), custom_call_target="tpu_custom_call" | custom-call | tf_op jit(solution)/shard_map/last/pallas_call | solution.py:908
  428.9 2.9 bitcast_convert_fusion
  431.7 0.7 slice.18
  432.5 0.6 fusion.2
  433.1 0.7 slice.21
  433.8 0.1 constant_dynamic-slice_fusion.1
  433.8 0.5 slice_bitcast_fusion
  434.4 0.0 copy-done.4
  434.4 1.6 bitcast_convert_fusion.1
  435.9 1.1 copy.24
  437.1 0.9 copy-done.5
  438.0 0.8 copy.25
  438.8 2.1 copy.26
  440.9 1.0 copy-done.2
  441.9 1.3 copy.27
  (9 shorter events, 0.0 us)
Async XLA Ops:
  0.6 161.5 %copy-start = (f32[256,2048]{1,0:T(8,128)S(1)}, f32[256,2048]{1,0:T(8,128)}, u32[]{:S(2)}) copy-start(f32[256,2048]{1,0:T(8,128)} %param.19) | copy-start | bytes 6291460
  428.8 5.5 %copy-start.4 = (bf16[1,256,2048]{2,1,0:T(8,128)(2,1)S(1)}, bf16[1,256,2048]{2,1,0:T(8,128)(2,1)}, u32[]{:S(2)}) copy-start(bf16[1,256,2048]{2,1,0:T(8,128)(2,1)} %get-tuple-element.41) | copy-start | bytes 3145732
  433.8 2.2 copy-start.3
  434.4 4.4 copy-start.1
  435.9 2.0 copy-start.5
  438.8 3.1 copy-start.2
where the time goes:
time: 444 us; the launch traced here: 443 us
  Pallas kernels  422 us (95%)
  local copies, waits for them, and re-layouts  15 us (3%)
  other arithmetic  5.79 us (1%)
    pallas_call x1, Pallas kernels, enter_call(): pl.pallas_call(functools.partial(enter_kernel, na, nb), out_shape=tuple(o...  156 us
    pallas_call x1, Pallas kernels, middle_call(): pl.pallas_call(functools.partial(middle_kernel, na, nb), out_shape=outs,...  137 us
    pallas_call x1, Pallas kernels, last_call(): pl.pallas_call(functools.partial(last_kernel, na, nb), out_shape=outs, in...  128 us

commit v1 on v0

--- a/solution.py
+++ b/solution.py
@@ -550,10 +550,15 @@
 
 
 def middle_kernel(na, nb, *refs):
-    x_ref, w_ref, res_ref, grad_ref, proj_ref, inv_ref, gain_ref = refs[:7]
+    x_ref, w_ref, res_ref, grad_far, proj_ref, inv_ref, gain_ref = refs[:7]
     block_ref, back_out, ffn_sum_ref, grad_res_ref, attn_sum_ref, down_sum_ref, gu_grad_ref = refs[7:14]
-    out, hidden_ref, grad_gu_ref, gu_ref, part_ref, down_grad, down_held = refs[14:21]
-    scratch, (send_sem, recv_sem) = refs[21:-2], refs[-2:]
+    out, hidden_ref, grad_gu_ref, gu_ref, part_ref, down_grad, down_held, grad_ref = refs[14:22]
+    scratch, (local_sem, send_sem, recv_sem) = refs[22:-3], refs[-3:]
+    share = 2 * lax.axis_index("q") + lax.axis_index("p")
+    load = pltpu.make_async_copy(
+        grad_far.at[:, span(share, grad_ref.shape[1])], grad_ref, local_sem.at[0]
+    )
+    load.start()
     units = hidden_ref.shape[2]
     width = x_ref.shape[2]
     b = lax.axis_index("b")
@@ -658,6 +663,7 @@
     }
     table.update({"r" + key: step for key, step in r.steps(first, second, 2).items()})
     table.update({"s" + key: step for key, step in s.steps(back_first, back_second, 1).items()})
+    load.wait()
     for key, *where in MIDDLE:
         table[key](*where)
     for h in range(HALVES):
@@ -667,11 +673,11 @@
     links.finish()
 
 
-def middle_call(nb, x_all, w_mlp, res_mine, grad_mine, proj_mine, inv_mine, width_gain):
+def middle_call(nb, x_all, w_mlp, res_mine, out_grad, proj_mine, inv_mine, width_gain):
     na, rows, width = x_all.shape
     quarter, units = width // 4, w_mlp.shape[1] // 3
     w_rows = width // (na * nb)
-    vmem = pl.BlockSpec(memory_space=pltpu.VMEM)
+    vmem, far = pl.BlockSpec(memory_space=pltpu.VMEM), pl.BlockSpec(memory_space=pl.ANY)
     shape = jax.ShapeDtypeStruct
     outs = (
         shape((1, rows, width), bf16),
@@ -686,7 +692,7 @@
     return pl.pallas_call(
         functools.partial(middle_kernel, na, nb),
         out_shape=outs,
-        in_specs=[vmem] * 7,
+        in_specs=[far if i == 3 else vmem for i in range(7)],
         out_specs=(vmem,) * len(outs),
         scratch_shapes=[
             pltpu.VMEM((na, rows, width), bf16),
@@ -696,15 +702,20 @@
             pltpu.VMEM((na, rows, width), bf16),
             pltpu.VMEM((na, nb, w_rows, units), bf16),
             pltpu.VMEM((nb - 1, na, w_rows, units), bf16),
+            pltpu.VMEM((rows, quarter), f32),
         ]
         + reduce_scratch(na, rows, width)
         + reduce_scratch(na, rows, width)
-        + [pltpu.SemaphoreType.DMA((copies,)), pltpu.SemaphoreType.DMA((copies,))],
+        + [
+            pltpu.SemaphoreType.DMA((1,)),
+            pltpu.SemaphoreType.DMA((copies,)),
+            pltpu.SemaphoreType.DMA((copies,)),
+        ],
         compiler_params=pltpu.CompilerParams(
             collective_id=2, has_side_effects=True, vmem_limit_bytes=VMEM_LIMIT
         ),
         name="middle",
-    )(x_all, w_mlp, res_mine, grad_mine, proj_mine, inv_mine, width_gain)
+    )(x_all, w_mlp, res_mine, out_grad, proj_mine, inv_mine, width_gain)
 
 
 def last_kernel(na, nb, *refs):
@@ -979,14 +990,14 @@
 )
 
 
-def enter_kernel(na, nb, *refs):
-    tok_ref, qkv_w_ref, wout_ref, gu_ref, down_ref, cos_ref, sin_ref = refs[:7]
-    gain_refs = refs[7:11]
-    x_far, w_far, mlp_w_ref, width_gain_ref, head_gain_ref, qkv_far, stats_ref, att_far = refs[11:19]
-    out, proj_ref, inv_ref, res_ref = refs[19:23]
-    own_gains, gains_ref, piece_ref, part_ref, held, stats_a = refs[23:29]
-    x_ref, w_ref, qkv_ref, att_ref = refs[29:33]
-    scratch, (local_sem, send_sem, recv_sem) = refs[33:-3], refs[-3:]
+def enter_kernel(na, nb, gain_sizes, *refs):
+    tok_far, qkv_w_ref, wout_ref, gu_ref, down_ref, cos_ref, sin_ref, all_gains_ref = refs[:8]
+    x_far, w_far, mlp_w_ref, width_gain_ref, head_gain_ref, qkv_far, stats_ref, att_far = refs[8:16]
+    out, proj_ref, inv_ref, res_ref = refs[16:20]
+    own_gains, gains_ref, piece_ref, part_ref, held, stats_a = refs[20:26]
+    x_ref, w_ref, qkv_ref, att_ref = refs[26:30]
+    tok_ref = refs[30]
+    scratch, (local_sem, send_sem, recv_sem) = refs[31:-3], refs[-3:]
     saves = [
         pltpu.make_async_copy(near, there, local_sem.at[5 + i])
         for i, (near, there) in enumerate(
@@ -996,16 +1007,24 @@
     a, b, p, q = (lax.axis_index(axis) for axis in ("a", "b", "p", "q"))
     rows = wout_ref.shape[0]
     quarter = tok_ref.shape[1]
+    load = pltpu.make_async_copy(
+        tok_far.at[:, span(2 * q + p, quarter)], tok_ref, local_sem.at[9]
+    )
+    load.start()
     units = down_ref.shape[1] // na
     own_gains[...] = jnp.zeros_like(own_gains)
-    for i, ref in enumerate(gain_refs):
-        own_gains[i : i + 1, : ref.shape[1]] = ref[...].astype(f32)
+    n_d, n_h = gain_sizes
+    place = 0
+    for i, size in enumerate((n_d, n_d, n_h, n_h)):
+        own_gains[i : i + 1, :size] = all_gains_ref[:, place : place + size].astype(f32)
+        place += size
     gains_ref[a, b] = own_gains[...]
     greet(
         [{"q": 1 - q}, {"p": 1 - p}]
         + [{"a": across(a, k)} for k in range(1, na)]
         + [{"b": across(b, j)} for j in range(1, nb)]
     )
+    load.wait()
     links = Links(send_sem, recv_sem)
     mine, pair = span(2 * q + p, quarter), span(q, 2 * quarter)
     place = span(a * nb + b, rows)
@@ -1114,7 +1133,6 @@
         over_heads.done()
         for copy in copies["gb"]:
             copy.wait_recv()
-        n_d, n_h = gain_refs[0].shape[1], gain_refs[2].shape[1]
         width_gain_ref[...] = jnp.zeros_like(width_gain_ref)
         head_gain_ref[...] = jnp.zeros_like(head_gain_ref)
         for i in range(2):
@@ -1178,11 +1196,12 @@
     links.finish()
 
 
-def enter_call(na, nb, tok_mine, qkv, w_out, gu, down, cos_table, sine_table, gains):
-    rows, quarter = tok_mine.shape
-    width = 4 * quarter
+def enter_call(na, nb, tokens, qkv, w_out, gu, down, cos_table, sine_table, gains):
+    rows, width = tokens.shape
+    quarter = width // 4
+    sizes = (gains[0].shape[0], gains[2].shape[0])
     w_rows, units = down.shape[0], down.shape[1] // na
-    lanes = max(128, gains[0].shape[1])
+    lanes = max(128, sizes[0])
     vmem, far = pl.BlockSpec(memory_space=pltpu.VMEM), pl.BlockSpec(memory_space=pl.ANY)
     shape = jax.ShapeDtypeStruct
     full = shape((na, rows, width), bf16)
@@ -1202,9 +1221,9 @@
     ]
     copies = 90 + 16 * nb
     return pl.pallas_call(
-        functools.partial(enter_kernel, na, nb),
+        functools.partial(enter_kernel, na, nb, sizes),
         out_shape=tuple(outs),
-        in_specs=[vmem] * 11,
+        in_specs=[far] + [vmem] * 7,
         out_specs=tuple(far if i in (0, 1, 5, 7) else vmem for i in range(len(outs))),
         scratch_shapes=[
             pltpu.VMEM((8, lanes), f32),
@@ -1217,10 +1236,11 @@
             pltpu.VMEM((width, 4 * HD), bf16),
             pltpu.VMEM((na, rows, 3 * HD), f32),
             pltpu.VMEM((na, rows, HD), bf16),
+            pltpu.VMEM((rows, quarter), bf16),
         ]
         + reduce_scratch(na, rows, width)
         + [
-            pltpu.SemaphoreType.DMA((9,)),
+            pltpu.SemaphoreType.DMA((10,)),
             pltpu.SemaphoreType.DMA((copies,)),
             pltpu.SemaphoreType.DMA((copies,)),
         ],
@@ -1228,7 +1248,7 @@
             collective_id=5, has_side_effects=True, vmem_limit_bytes=VMEM_LIMIT
         ),
         name="enter",
-    )(tok_mine, qkv, w_out, gu, down, cos_table, sine_table, *gains)
+    )(tokens, qkv, w_out, gu, down, cos_table, sine_table, jnp.concatenate(gains)[None])
 
 
 def rope_tables(length, width):
@@ -1260,10 +1280,6 @@
     w_rows = out_weight.shape[0]
     units = down_weight.shape[1] // na
 
-    def quarter_of(operand):
-        return lax.dynamic_slice_in_dim(operand, share * quarter, quarter, 1)
-
-    tok_mine, grad_mine = quarter_of(tokens), quarter_of(out_grad)
     cos_table, sine_table = rope_tables(SEQ_LEN, HD)
     (
         x_all,
@@ -1281,18 +1297,18 @@
     ) = enter_call(
         na,
         nb,
-        tok_mine,
+        tokens,
         qkv_weight.transpose(1, 0, 2),
         out_weight,
         gu_weight,
         down_weight,
         cos_table,
         sine_table,
-        [gain[None] for gain in (attn_gain, ffn_gain, q_gain, k_gain)],
+        (attn_gain, ffn_gain, q_gain, k_gain),
     )
     n_d, n_h = attn_gain.shape[0], q_gain.shape[0]
     block_rows, grad_proj, ffn_sums, grad_res, attn_sums, down_sum, gu_grad = middle_call(
-        nb, res_all, w_mlp, res_mine, grad_mine, proj_mine, inv_mine, width_gain
+        nb, res_all, w_mlp, res_mine, out_grad, proj_mine, inv_mine, width_gain
     )
     grad_rows, sums, down_grad, gu_grad, qkv_grad, out_grad_w = last_call(
         nb,

time: 444 us -> 440 us (level)
  no operation moved by 1% of the time
where the time goes in v1:
time: 440 us
  Pallas kernels  422 us (96%)
  local copies, waits for them, and re-layouts  10.6 us (2%)
  other arithmetic  6.57 us (1%)
    pallas_call x1, Pallas kernels, enter_call(): pl.pallas_call(functools.partial(enter_kernel, na, nb, sizes), out_shape=...  157 us
    pallas_call x1, Pallas kernels, middle_call(): pl.pallas_call(functools.partial(middle_kernel, na, nb), out_shape=outs,...  135 us
    pallas_call x1, Pallas kernels, last_call(): pl.pallas_call(functools.partial(last_kernel, na, nb), out_shape=outs, in...  130 us

profile of v1, /device:TPU:8, one launch (start us, length us, event | category | flops | bytes accessed | tf_op | source)
XLA Modules:
  0.0 440.1 jit_solution(7873961053349784218)
XLA Ops:
  0.7 0.5 fusion
  1.2 0.8 pad_maximum_fusion
  2.0 0.8 pad_maximum_fusion.2
  2.8 0.6 broadcast_in_dim.2.refs_7_
  3.4 156.6 %enter.1 = (bf16[4,256,2048]{2,1,0:T(8,128)(2,1)}, bf16[2048,512]{1,0:T(8,128)(2,1)}, bf16[2048,1536]{1,0:T(8,128)(2,1)}, f32[8,512]{1,0:T(8,128)}, f32[8,128]{1...) custom-call(bf16[256,2048]{1,0:T(8,128)(2,1)} %refs_0_.1, ...), custom_call_target="tpu_custom_call" | custom-call | tf_op jit(solution)/shard_map/enter/pallas_call | solution.py:1223
  160.0 135.4 %middle.1 = (bf16[1,256,2048]{2,1,0:T(8,128)(2,1)}, bf16[4,256,2048]{2,1,0:T(8,128)(2,1)}, f32[8,512]{1,0:T(8,128)}, f32[256,512]{1,0:T(8,128)}, f32[8,512]{1,0:...) custom-call(bf16[4,256,2048]{2,1,0:T(8,128)(2,1)} %get-tuple-element.35.refs_0_, ...), custom_call_target="tpu_custom_call" | custom-call | tf_op jit(solution)/shard_map/middle/pallas_call | solution.py:692
  295.4 130.2 %last.1 = (bf16[1,256,2048]{2,1,0:T(8,128)(2,1)}, f32[8,640]{1,0:T(8,128)}, f32[256,2048]{1,0:T(8,128)}, f32[256,2,2048]{2,1,0:T(2,128)}, f32[3,256,512]{2,1,0:T(8,128)}, /*index=5*/f32[256,512]{1,0:T(8,128)}) custom-call(bf16[4,256,2048]{2,1,0:T(8,128)(2,1)} %get-tuple-element.42.refs_0_, bf16[4,256,2048]{2,1,0:T(8,128)(2,1)} %get-tuple-element.43.refs_1_, ...), custom_call_target="tpu_custom_call" | custom-call | tf_op jit(solution)/shard_map/last/pallas_call | solution.py:919
  425.6 0.0 copy-start.3
  425.6 2.9 bitcast_convert_fusion
  428.5 0.8 slice.18
  429.3 0.6 fusion.2
  429.9 0.7 slice.21
  430.6 0.1 constant_dynamic-slice_fusion.1
  430.7 0.5 slice_bitcast_fusion
  431.2 0.0 copy-done.3
  431.2 1.6 bitcast_convert_fusion.1
  432.8 0.0 copy-done.2
  432.8 1.1 copy.24
  433.9 0.9 copy-done.4
  434.8 0.8 copy.25
  435.6 0.0 copy-done
  435.6 2.1 copy.26
  437.8 1.0 copy-done.1
  438.7 1.3 copy.27
  (5 shorter events, 0.0 us)
Async XLA Ops:
  425.6 5.6 %copy-start.3 = (bf16[1,256,2048]{2,1,0:T(8,128)(2,1)S(1)}, bf16[1,256,2048]{2,1,0:T(8,128)(2,1)}, u32[]{:S(2)}) copy-start(bf16[1,256,2048]{2,1,0:T(8,128)(2,1)} %get-tuple-element.41) | copy-start | bytes 3145732
  428.5 4.3 copy-start.2
  431.2 4.4 %copy-start = (f32[256,2,2048]{2,1,0:T(2,128)S(1)}, f32[256,2,2048]{2,1,0:T(2,128)}, u32[]{:S(2)}) copy-start(f32[256,2,2048]{2,1,0:T(2,128)} %get-tuple-element.82) | copy-start | bytes 12582916
  432.8 2.1 copy-start.4
  435.6 3.1 copy-start.1

commit v2 on v1

--- a/solution.py
+++ b/solution.py
@@ -19,7 +19,7 @@
 bf16 = jnp.bfloat16
 MESH = pl.DeviceIdType.MESH
 EXACT = lax.Precision.HIGHEST
-VMEM_LIMIT = 60 * 1024 * 1024
+VMEM_LIMIT = 63 * 1024 * 1024
 TILE = 32
 HALVES = 2
 
@@ -170,7 +170,7 @@
     return queries, key_rows, values, q_inv, k_inv, q_rot, k_rot, probs
 
 
-def weight_grad(left, right, out, block, columns=None):
+def weight_grad(left, right, out, block, columns=None, take=slice(None)):
     na, nb, rows = left.shape[0], out.shape[1], out.shape[2]
     columns = columns or slice(0, right.shape[2])
     size = max(rows, 256)
@@ -178,9 +178,9 @@
 
     def chunk(i, carry):
         at = span(block * (nb * rows // size) + i, size)
-        total = t_dot(left[0, :, at], right[0])
+        total = t_dot(left[0, :, at], right[0, :, take])
         for k in range(1, na):
-            total = total + t_dot(left[k, :, at], right[k])
+            total = total + t_dot(left[k, :, at], right[k, :, take])
         for j in range(size // rows):
             part = total[j * rows : (j + 1) * rows].astype(bf16)
             out[block, i * (size // rows) + j, :, columns] = part
@@ -191,9 +191,10 @@
 
 def exchange_b(links, grad, held, columns):
     b = lax.axis_index("b")
+    put = columns if held.shape[3] == grad.shape[3] or columns.stop <= held.shape[3] else slice(None)
     return [
         links.send(
-            grad.at[:, across(b, j), :, columns], held.at[j - 1, :, :, columns], {"b": across(b, j)}
+            grad.at[:, across(b, j), :, columns], held.at[j - 1, :, :, put], {"b": across(b, j)}
         )
         for j in range(1, held.shape[0] + 1)
     ]
@@ -282,6 +283,7 @@
         self.lead = list(range(2, na)) + [1, 0]
         self.step_q, self.step_p, self.step_a = {}, {}, {}
         self.spread_a, self.spread_p, self.spread_q, self.stats = {}, {}, {}, {}
+        self.here = set()
 
     def at(self, h):
         return slice(h * self.count, (h + 1) * self.count)
@@ -380,7 +382,9 @@
         self.spread_q[h, k] = self.links.send(here, here, {"q": 1 - self.q})
 
     def arrived(self, h, k):
-        self.spread_q[h, k].wait_recv()
+        if (h, k) not in self.here:
+            self.here.add((h, k))
+            self.spread_q[h, k].wait_recv()
 
     def steps(self, first, second, number, chain=False):
         def normed(h):
@@ -532,28 +536,31 @@
 
 
 MIDDLE = (
-    ("F", 2), ("rP", 0, 2), ("F", 3), ("rP", 0, 3), ("rA", 0, 2), ("rP", 1, 3), ("rP", 1, 2), ("F", 1),
-    ("rA", 0, 3), ("F", 0), ("rP", 0, 1), ("rA", 1, 3), ("rP", 1, 1), ("rP", 0, 0), ("rA", 1, 2),
-    ("rP", 1, 0), ("rA", 0, 1), ("rA", 1, 1), ("rSC", 0), ("rSQ", 0), ("rSC", 1), ("rSD", 0), ("rZ", 0, 3),
-    ("rX", 0), ("rSQ", 1), ("rSD", 1), ("rZ", 0, 1), ("BP",), ("rZ", 1, 3), ("rZ", 0, 2), ("rZ", 1, 1),
-    ("rRP", 0, 3), ("rX", 1), ("rRP", 0, 1), ("rZ", 1, 2), ("rRQ", 0, 3), ("B", 0, 3), ("rRP", 0, 2),
-    ("rRP", 1, 3), ("sP", 0, 3), ("rRQ", 0, 1), ("rRP", 1, 2), ("rRQ", 0, 2), ("rRQ", 1, 3), ("rRP", 1, 1),
-    ("B", 0, 2), ("B", 0, 1), ("rRQ", 0, 0), ("sP", 0, 2), ("B", 1, 3), ("sP", 0, 1), ("rRQ", 1, 2),
-    ("sA", 0, 3), ("B", 0, 0), ("sP", 1, 3), ("rRQ", 1, 1), ("sA", 0, 2), ("rRQ", 1, 0), ("B", 1, 2),
-    ("sP", 0, 0), ("sA", 0, 1), ("B", 1, 1), ("sP", 1, 2), ("B", 1, 0), ("sA", 1, 3), ("sP", 1, 1),
-    ("sSC", 0), ("sA", 1, 2), ("BQ",), ("sP", 1, 0), ("sSQ", 0), ("sA", 1, 1), ("sSD", 0), ("sZ", 0, 2),
-    ("D",), ("sX", 0), ("sZ", 0, 1), ("sSC", 1), ("sSQ", 1), ("sZ", 0, 3), ("sRP", 0, 2), ("sSD", 1),
-    ("sZ", 1, 1), ("sRP", 0, 1), ("sX", 1), ("sRQ", 0, 0), ("G", 2), ("sZ", 1, 3), ("G", 3), ("G", 1),
-    ("sRP", 0, 3), ("G", 0), ("sZ", 1, 2), ("sRP", 1, 3), ("sRQ", 0, 1), ("sRQ", 1, 0), ("sRP", 1, 1),
-    ("sRP", 1, 2), ("sRQ", 0, 2), ("sRQ", 0, 3), ("sRQ", 1, 3), ("sRQ", 1, 1), ("DS",), ("sRQ", 1, 2),
+    ("F", 2), ("F", 3), ("rP", 0, 2), ("F", 1), ("rP", 0, 3), ("rA", 0, 2), ("rP", 0, 1), ("rP", 1, 3),
+    ("F", 0), ("rP", 1, 2), ("rA", 0, 3), ("rP", 1, 1), ("rA", 0, 1), ("rP", 0, 0), ("rA", 1, 3),
+    ("rA", 1, 1), ("rA", 1, 2), ("rSC", 0), ("rP", 1, 0), ("rSQ", 0), ("rSD", 0), ("rZ", 0, 1), ("rX", 0),
+    ("rZ", 0, 3), ("rSC", 1), ("rRP", 0, 1), ("rRQ", 0, 0), ("rSQ", 1), ("rZ", 0, 2), ("rSD", 1),
+    ("rRP", 0, 3), ("rX", 1), ("rZ", 1, 1), ("rZ", 1, 2), ("rRP", 0, 2), ("rRQ", 0, 1), ("rRQ", 0, 3),
+    ("rRP", 1, 1), ("B", 0, 3), ("rZ", 1, 3), ("rRP", 1, 2), ("rRQ", 1, 0), ("B", 0, 1), ("rRQ", 0, 2),
+    ("sP", 0, 3), ("B", 0, 0), ("B", 0, 2), ("rRP", 1, 3), ("rRQ", 1, 2), ("sA", 0, 3), ("sP", 0, 2),
+    ("B", 1, 2), ("sP", 0, 1), ("rRQ", 1, 1), ("rRQ", 1, 3), ("sA", 0, 2), ("sP", 1, 2), ("D", 0),
+    ("sA", 0, 1), ("B", 1, 3), ("sA", 1, 2), ("sP", 1, 3), ("B", 1, 0), ("sP", 0, 0), ("D", 1),
+    ("sA", 1, 3), ("sP", 1, 0), ("B", 1, 1), ("sSC", 0), ("sP", 1, 1), ("DS", 0), ("ZD", 0, 2), ("sSQ", 0),
+    ("G", 0), ("sSD", 0), ("BP",), ("sA", 1, 1), ("G", 2), ("sZ", 0, 3), ("G", 3), ("sZ", 0, 2), ("sSC", 1),
+    ("G", 1), ("YG",), ("sSQ", 1), ("sRP", 0, 3), ("sSD", 1), ("sZ", 1, 3), ("DS", 1), ("sZ", 1, 1),
+    ("sZ", 0, 1), ("BQ",), ("sX", 0), ("ZD", 1, 3), ("sRP", 1, 1), ("sX", 1), ("sRQ", 1, 1), ("sZ", 1, 2),
+    ("sRP", 0, 2), ("sRP", 0, 1), ("ZD", 0, 1), ("ZD", 1, 1), ("sRP", 1, 2), ("sRP", 1, 3), ("ZD", 1, 2),
+    ("sRQ", 0, 0), ("sRQ", 0, 3), ("ZD", 0, 3), ("sRQ", 1, 0), ("sRQ", 1, 2), ("sRQ", 0, 2), ("sRQ", 0, 1),
+    ("sRQ", 1, 3), ("SG",),
 )
 
 
 def middle_kernel(na, nb, *refs):
     x_ref, w_ref, res_ref, grad_far, proj_ref, inv_ref, gain_ref = refs[:7]
     block_ref, back_out, ffn_sum_ref, grad_res_ref, attn_sum_ref, down_sum_ref, gu_grad_ref = refs[7:14]
-    out, hidden_ref, grad_gu_ref, gu_ref, part_ref, down_grad, down_held, grad_ref = refs[14:22]
-    scratch, (local_sem, send_sem, recv_sem) = refs[22:-3], refs[-3:]
+    down_in, gate_sum_ref = refs[14:16]
+    out, hidden_ref, grad_gu_ref, gu_ref, part_ref, down_grad, down_held, grad_ref, gu_held = refs[16:25]
+    scratch, (local_sem, send_sem, recv_sem) = refs[25:-3], refs[-3:]
     share = 2 * lax.axis_index("q") + lax.axis_index("p")
     load = pltpu.make_async_copy(
         grad_far.at[:, span(share, grad_ref.shape[1])], grad_ref, local_sem.at[0]
@@ -621,7 +628,10 @@
         s, grad_ref, proj_ref, inv_ref, gain_ref, grad_res_ref, attn_sum_ref
     )
     copies, reused = {}, []
-    columns = slice(0, units)
+    gate = slice(0, units)
+
+    def half(c):
+        return slice(c * units // 2, (c + 1) * units // 2)
 
     def forward_step(k):
         forward(k)
@@ -645,10 +655,25 @@
         here = block_ref.at[0, :, r.pair]
         copies["q"] = links.send(here, here, {"q": 1 - r.q})
 
-    def down_grads():
+    def down_grads(c):
+        for h in range(HALVES):
+            for k in range(na):
+                r.arrived(h, k)
         for block in range(na):
-            weight_grad(out, hidden_ref, down_grad, block)
-        copies["b"] = exchange_b(links, down_grad, down_held, columns)
+            weight_grad(out, hidden_ref, down_grad, block, half(c), half(c))
+        copies["d", c] = exchange_b(links, down_grad, down_held, half(c))
+
+    def down_sums(c):
+        own = lambda block: down_grad.at[block, b]
+        sum_b(copies["d", c], own, down_held, down_sum_ref, half(c))
+
+    def down_owner(c, k):
+        copies["z", c, k] = links.send(
+            down_sum_ref.at[across(r.a, k), :, half(c)], down_in.at[k - 1, :, half(c)], {"a": across(r.a, k)}
+        )
+
+    def gate_rows():
+        copies["g"] = exchange_b(links, gu_grad_ref, gu_held, gate)
 
     table = {
         "F": forward_step,
@@ -656,8 +681,11 @@
         "BP": block_p,
         "BQ": block_q,
         "D": down_grads,
-        "DS": lambda: sum_b(
-            copies["b"], lambda block: down_grad.at[block, b], down_held, down_sum_ref, columns
+        "DS": down_sums,
+        "ZD": down_owner,
+        "YG": gate_rows,
+        "SG": lambda: sum_b(
+            copies["g"], lambda block: gu_grad_ref.at[block, b], gu_held, gate_sum_ref, gate
         ),
         "G": lambda block: weight_grad(x_ref, grad_gu_ref, gu_grad_ref, block),
     }
@@ -670,6 +698,9 @@
         for k in range(na):
             s.arrived(h, k)
     copies["q"].wait_recv()
+    for c in range(2):
+        for k in range(1, na):
+            copies["z", c, k].wait_recv()
     links.finish()
 
 
@@ -687,8 +718,10 @@
         shape((8, quarter), f32),
         shape((na, w_rows, units), bf16),
         shape((na, nb, w_rows, 2 * units), bf16),
-    )
-    copies = 2 * HALVES * (6 * na + 1) + 2 + nb
+        shape((na - 1, w_rows, units), bf16),
+        shape((na, w_rows, units), bf16),
+    )
+    copies = 2 * HALVES * (6 * na + 1) + 2 + 3 * nb + 2 * na
     return pl.pallas_call(
         functools.partial(middle_kernel, na, nb),
         out_shape=outs,
@@ -703,6 +736,7 @@
             pltpu.VMEM((na, nb, w_rows, units), bf16),
             pltpu.VMEM((nb - 1, na, w_rows, units), bf16),
             pltpu.VMEM((rows, quarter), f32),
+            pltpu.VMEM((nb - 1, na, w_rows, units), bf16),
         ]
         + reduce_scratch(na, rows, width)
         + reduce_scratch(na, rows, width)
@@ -718,21 +752,37 @@
     )(x_all, w_mlp, res_mine, out_grad, proj_mine, inv_mine, width_gain)
 
 
+LAST = (
+    ("ZG", 0, 2), ("U1",), ("YG", 1), ("AB", 0), ("U2",), ("AB", 1), ("ZG", 0, 1), ("AB", 2),
+    ("WO", 3), ("U3",), ("ZG", 0, 3), ("AB", 3), ("OD", 2), ("S1",), ("S2",), ("S3",), ("WO", 0),
+    ("SG", 1), ("ZG", 1, 2), ("S4",), ("QB", 1), ("QB", 0), ("QB", 2), ("QB", 3), ("U4",), ("OWNG",),
+    ("OG", 0, 3), ("WQ", 1), ("ZG", 1, 3), ("rP", 1, 3), ("WQ", 2), ("rP", 0, 0), ("ZG", 1, 1),
+    ("OG", 0, 1), ("rP", 1, 2), ("rP", 0, 1), ("WQ", 0), ("rP", 1, 0), ("WO", 1), ("rA", 1, 3),
+    ("WO", 2), ("WQ", 3), ("YA",), ("OG", 0, 2), ("OD", 1), ("rP", 0, 2), ("rA", 1, 2), ("rA", 0, 1),
+    ("OG", 1, 1), ("OG", 1, 2), ("rA", 0, 2), ("rP", 1, 1), ("rP", 0, 3), ("rA", 1, 1), ("OD", 3),
+    ("rA", 0, 3), ("OG", 1, 3), ("rSC", 1), ("SA",), ("ZA", 2), ("U5",), ("rSC", 0), ("rX", 0), ("ZA", 3),
+    ("ZA", 1), ("OWN",), ("rX", 1), ("rRQ", 0, 0), ("OA", 2), ("OA", 1), ("rRQ", 1, 0),
+    ("OA", 3),
+)
+
+
 def last_kernel(na, nb, *refs):
     proj_ref, x_far, qkv_ref, stats_ref, gain_ref, cos_ref, sin_ref, w_ref, att_ref = refs[:9]
-    grad_ref, attn_sum_ref, ffn_sum_ref, down_sum_ref, gu_grad_far = refs[9:14]
-    out, sums_ref, down_far, gu_far, qkv_out, wout_out = refs[14:20]
-    scaled_ref, grad_qkv_ref, part_ref, head_sums, held, stats_a, inner_ref = refs[20:27]
-    own_sums, a_sums, b_sums, gu_held, gu_sum, attn_grad, attn_held, attn_sum = refs[27:35]
-    down_in, gu_in, attn_in, x_ref, gu_own, down_out, gu_out = refs[35:42]
-    scratch, (local_sem, send_sem, recv_sem) = refs[42:-3], refs[-3:]
+    grad_ref, attn_sum_ref, ffn_sum_ref, down_sum_ref, gu_grad_far, down_in, gate_ref = refs[9:16]
+    out, sums_ref, down_far, gu_far, qkv_out, wout_out = refs[16:22]
+    scaled_ref, grad_qkv_ref, part_ref, head_sums, held, stats_a, inner_ref = refs[22:29]
+    own_sums, a_sums, b_sums, up_held, up_sum, attn_grad, attn_held, attn_sum = refs[29:37]
+    gu_in, attn_in, x_ref, up_own, down_out, gu_out = refs[37:43]
+    scratch, (local_sem, send_sem, recv_sem) = refs[43:-3], refs[-3:]
     links = Links(send_sem, recv_sem)
     load_gu = pltpu.make_async_copy(
-        gu_grad_far.at[:, lax.axis_index("b")], gu_own, local_sem.at[0]
+        gu_grad_far.at[:, lax.axis_index("b"), :, gate_ref.shape[2] :], up_own, local_sem.at[0]
     )
     load_gu.start()
     load_x = pltpu.make_async_copy(x_far, x_ref, local_sem.at[1])
     load_x.start()
+    save_down = pltpu.make_async_copy(down_out, down_far, local_sem.at[2])
+    save_gu = pltpu.make_async_copy(gu_out, gu_far, local_sem.at[3])
     r = Reduce(na, links, part_ref, out, scratch)
     a, b, p, q, mine, pair, quarter = (
         r.a, lax.axis_index("b"), r.p, r.q, r.mine, r.pair, r.quarter,
@@ -741,28 +791,57 @@
     own_sums[...] = jnp.zeros_like(own_sums)
     own_sums[0:1, mine] = jnp.sum(attn_sum_ref[...], axis=0, keepdims=True)
     own_sums[1:2, mine] = jnp.sum(ffn_sum_ref[...], axis=0, keepdims=True)
-    greet(reduce_peers(na) + [{"b": across(b, j)} for j in range(1, nb)])
-    far = list(range(2, na)) + [1]
-
-    def to_owners(source, target, columns):
-        return [
-            (k, links.send(
-                source.at[across(a, k), :, columns], target.at[k - 1, :, columns], {"a": across(a, k)}
-            ))
-            for k in far
-        ]
-
-    whole = slice(0, units)
-    halves = [slice(0, units), slice(units, 2 * units)]
-    down_copies = to_owners(down_sum_ref, down_in, whole)
-    gu_b = [exchange_b(links, gu_grad_far, gu_held, columns) for columns in halves]
-    here = own_sums.at[:, mine]
-    sums_p = links.send(here, here, {"p": 1 - p})
-
     held[0] = jnp.zeros_like(held[0])
     head_sums[...] = jnp.zeros_like(head_sums)
-
-    def attend_back(k, carry):
+    greet(reduce_peers(na) + [{"b": across(b, j)} for j in range(1, nb)])
+    copies, stored = {}, []
+    whole, upper = slice(0, units), slice(units, 2 * units)
+    attn_columns = slice(0, 4 * HD)
+    over_heads = OverHeads(links, na, a, p, q, held, stats_a, inner_ref)
+
+    def sums_pair():
+        here = own_sums.at[:, mine]
+        copies["u"] = links.send(here, here, {"p": 1 - p})
+
+    def sums_core():
+        copies["u"].wait_recv()
+        here = own_sums.at[:, pair]
+        copies["u"] = links.send(here, here, {"q": 1 - q})
+
+    def sums_far():
+        copies["u"].wait_recv()
+        copies["u"] = [
+            links.send(
+                own_sums.at[:, span(across(a, k), quarter)], a_sums.at[k - 1], {"a": across(a, k)}
+            )
+            for k in range(1, na)
+        ]
+
+    def sums_b():
+        for copy in copies["u"]:
+            copy.wait_recv()
+        total = own_sums[:, span(a, quarter)]
+        for k in range(1, na):
+            total = total + a_sums[k - 1]
+        b_sums[0, :, :quarter] = total
+        b_sums[0, :, quarter:] = head_sums[...]
+        copies["u"] = [
+            links.send(b_sums.at[0], b_sums.at[j], {"b": across(b, j)}) for j in range(1, nb)
+        ]
+
+    def sums_done():
+        for copy in copies["u"]:
+            copy.wait_recv()
+        total = b_sums[0]
+        for j in range(1, nb):
+            total = total + b_sums[j]
+        sums_ref[...] = total
+
+    def attend_back(k):
+        if k % 2 == 0:
+            lax.fori_loop(k, k + 2, attend_back_block, 0)
+
+    def attend_back_block(k, carry):
         queries, key_rows, values, q_inv, k_inv, q_rot, k_rot, probs = attention(
             k, qkv_ref[k], stats_ref[...], gain_ref, cos_ref, sin_ref
         )
@@ -786,26 +865,6 @@
         held[0] += to_row(scaled_q * queries, 2 * k) + to_row(scaled_k * key_rows, 2 * k + 1)
         return carry
 
-    lax.fori_loop(0, na, attend_back, 0)
-    sums_p.wait_recv()
-    here = own_sums.at[:, pair]
-    sums_q = links.send(here, here, {"q": 1 - q})
-    gu_copies = []
-
-    def sent():
-        for block in range(na):
-            weight_grad(proj_ref, att_ref, attn_grad, block, slice(3 * HD, 4 * HD))
-        load_gu.wait()
-        sum_b(gu_b[0], lambda block: gu_own.at[block], gu_held, gu_sum, halves[0])
-        gu_copies.append(to_owners(gu_sum, gu_in, halves[0]))
-
-    over_heads = OverHeads(links, na, a, p, q, held, stats_a, inner_ref)
-    over_heads.to_pair()
-    over_heads.to_core()
-    over_heads.to_all()
-    sent()
-    over_heads.done()
-
     def qkv_back(k):
         for i in range(2):
             at = slice(i * HD, (i + 1) * HD)
@@ -820,80 +879,106 @@
             return carry
 
         lax.fori_loop(0, part_ref.shape[2] // 512, part, 0)
-
-    for k in r.lead:
-        qkv_back(k)
         for h in range(HALVES):
             r.send_q(h, k)
-    for h in range(HALVES):
-        for k in r.lead:
-            r.send_p(h, k)
-    load_x.wait()
-    for block in range(na):
+
+    def qkv_grads(block):
+        if "x" not in copies:
+            load_x.wait()
+            copies["x"] = True
         weight_grad(x_ref, grad_qkv_ref, attn_grad, block, slice(0, 3 * HD))
-    attn_columns = slice(0, 4 * HD)
-    attn_b = exchange_b(links, attn_grad, attn_held, attn_columns)
-    for h in range(HALVES):
-        for k in r.lead:
-            r.send_a(h, k)
-    sums_q.wait_recv()
-    sums_a = [
-        links.send(own_sums.at[:, span(across(a, k), quarter)], a_sums.at[k - 1], {"a": across(a, k)})
-        for k in range(1, na)
-    ]
-    sum_b(gu_b[1], lambda block: gu_own.at[block], gu_held, gu_sum, halves[1])
-    gu_copies.append(to_owners(gu_sum, gu_in, halves[1]))
+
+    def up_rows(_):
+        copies["up"] = exchange_b(links, gu_grad_far, up_held, upper)
+
+    def up_sums(_):
+        load_gu.wait()
+        own = lambda block: up_own.at[block]
+        sum_b(copies["up"], own, up_held, up_sum, whole)
+
+    def gu_owner(c, k):
+        source = up_sum if c else gate_ref
+        copies["g", c, k] = links.send(
+            source.at[across(a, k)], gu_in.at[k - 1, c], {"a": across(a, k)}
+        )
+
+    def attn_rows():
+        copies["at"] = exchange_b(links, attn_grad, attn_held, attn_columns)
+
+    def attn_sums():
+        own = lambda block: attn_grad.at[block, b]
+        sum_b(copies["at"], own, attn_held, attn_sum, attn_columns)
+
+    def attn_owner(k):
+        copies["a", k] = links.send(attn_sum.at[across(a, k)], attn_in.at[k - 1], {"a": across(a, k)})
+
+    def store(target, index, size, value):
+        target[:, span(index, size)] = value.astype(f32)
+
+    def store_gu(c, k, value):
+        gu_out[:, c, span(across(a, k), units)] = value.astype(f32)
+        stored.append((c, k))
+        if len(stored) == 2 * na:
+            save_gu.start()
+
+    def store_attn(k, values):
+        for c in range(3):
+            store(qkv_out.at[c], across(a, k), HD, values[:, c * HD : (c + 1) * HD])
+        store(wout_out, across(a, k), HD, values[:, 3 * HD :])
+
+    def own_gu():
+        store_gu(0, 0, gate_ref[a])
+        store_gu(1, 0, up_sum[a])
+
+    def gu_arrived(c, k):
+        copies["g", c, k].wait_recv()
+        store_gu(c, k, gu_in[k - 1, c])
+
+    def attn_arrived(k):
+        copies["a", k].wait_recv()
+        store_attn(k, attn_in[k - 1])
+
+    def down_rows(k):
+        if "down" not in copies:
+            copies["down"] = 0
+            store(down_out, a, units, down_sum_ref[a])
+        store(down_out, across(a, k), units, down_in[k - 1])
+        copies["down"] += 1
+        if copies["down"] == na - 1:
+            save_down.start()
 
     def first(at):
         out[0, at, mine] = (grad_ref[at] + r.add_all(at)).astype(bf16)
 
-    for h in range(HALVES):
-        r.scattered(h, first, 0)
-        r.spread(h, [0])
-    for copy in sums_a:
-        copy.wait_recv()
-    total = own_sums[:, span(a, quarter)]
-    for k in range(1, na):
-        total = total + a_sums[k - 1]
-    b_sums[0, :, :quarter] = total
-    b_sums[0, :, quarter:] = head_sums[...]
-    sums_b = [links.send(b_sums.at[0], b_sums.at[j], {"b": across(b, j)}) for j in range(1, nb)]
-    for h in range(HALVES):
-        r.relay_q(h, 0)
-    sum_b(attn_b, lambda block: attn_grad.at[block, b], attn_held, attn_sum, attn_columns)
-    attn_copies = to_owners(attn_sum, attn_in, attn_columns)
-
-    def store(target, index, size, value):
-        target[:, span(index, size)] = value.astype(f32)
-
-    store(down_out, a, units, down_sum_ref[a])
-    for c in range(2):
-        gu_out[:, c, span(a, units)] = gu_sum[a, :, halves[c]].astype(f32)
-    for c in range(3):
-        store(qkv_out.at[c], a, HD, attn_sum[a, :, c * HD : (c + 1) * HD])
-    store(wout_out, a, HD, attn_sum[a, :, 3 * HD :])
-    for k, copy in down_copies:
-        copy.wait_recv()
-        store(down_out, across(a, k), units, down_in[k - 1])
-    save_down = pltpu.make_async_copy(down_out, down_far, local_sem.at[2])
-    save_down.start()
-    for copy in sums_b:
-        copy.wait_recv()
-    total = b_sums[0]
-    for j in range(1, nb):
-        total = total + b_sums[j]
-    sums_ref[...] = total
-    for c in range(2):
-        for k, copy in gu_copies[c]:
-            copy.wait_recv()
-            gu_out[:, c, span(across(a, k), units)] = gu_in[k - 1, :, halves[c]].astype(f32)
-    save_gu = pltpu.make_async_copy(gu_out, gu_far, local_sem.at[3])
-    save_gu.start()
-    for k, copy in attn_copies:
-        copy.wait_recv()
-        for c in range(3):
-            store(qkv_out.at[c], across(a, k), HD, attn_in[k - 1, :, c * HD : (c + 1) * HD])
-        store(wout_out, across(a, k), HD, attn_in[k - 1, :, 3 * HD :])
+    table = {
+        "U1": sums_pair,
+        "U2": sums_core,
+        "U3": sums_far,
+        "U4": sums_b,
+        "U5": sums_done,
+        "AB": attend_back,
+        "S1": over_heads.to_pair,
+        "S2": over_heads.to_core,
+        "S3": over_heads.to_all,
+        "S4": over_heads.done,
+        "WO": lambda block: weight_grad(proj_ref, att_ref, attn_grad, block, slice(3 * HD, 4 * HD)),
+        "WQ": qkv_grads,
+        "QB": qkv_back,
+        "YG": up_rows,
+        "SG": up_sums,
+        "ZG": gu_owner,
+        "YA": attn_rows,
+        "SA": attn_sums,
+        "ZA": attn_owner,
+        "OWNG": own_gu,
+        "OWN": lambda: store_attn(0, attn_sum[a]),
+        "OD": down_rows,
+        "OG": gu_arrived,
+        "OA": attn_arrived,
+    }
+    table.update({"r" + key: step for key, step in r.steps(first, None, 0).items()})
+    for key, *where in LAST:
+        table[key](*where)
     for h in range(HALVES):
         r.arrived(h, 0)
     save_down.wait()
@@ -919,7 +1004,7 @@
     return pl.pallas_call(
         functools.partial(last_kernel, na, nb),
         out_shape=outs,
-        in_specs=[far if i in (1, 13) else vmem for i in range(14)],
+        in_specs=[far if i in (1, 13) else vmem for i in range(16)],
         out_specs=(vmem, vmem, far, far, vmem, vmem),
         scratch_shapes=[
             pltpu.VMEM((na, rows, 2 * HD), f32),
@@ -932,16 +1017,15 @@
             pltpu.VMEM((8, width), f32),
             pltpu.VMEM((na - 1, 8, quarter), f32),
             pltpu.VMEM((nb, 8, quarter + HD), f32),
-            pltpu.VMEM((nb - 1, na, w_rows, 2 * units), bf16),
-            pltpu.VMEM((na, w_rows, 2 * units), bf16),
+            pltpu.VMEM((nb - 1, na, w_rows, units), bf16),
+            pltpu.VMEM((na, w_rows, units), bf16),
             pltpu.VMEM((na, nb, w_rows, 4 * HD), bf16),
             pltpu.VMEM((nb - 1, na, w_rows, 4 * HD), bf16),
             pltpu.VMEM((na, w_rows, 4 * HD), bf16),
-            pltpu.VMEM((na - 1, w_rows, units), bf16),
-            pltpu.VMEM((na - 1, w_rows, 2 * units), bf16),
+            pltpu.VMEM((na - 1, 2, w_rows, units), bf16),
             pltpu.VMEM((na - 1, w_rows, 4 * HD), bf16),
             pltpu.VMEM((na, rows, width), bf16),
-            pltpu.VMEM((na, w_rows, 2 * units), bf16),
+            pltpu.VMEM((na, w_rows, units), bf16),
             pltpu.VMEM((w_rows, na * units), f32),
             pltpu.VMEM((w_rows, 2, na * units), f32),
         ]
@@ -1307,7 +1391,7 @@
         (attn_gain, ffn_gain, q_gain, k_gain),
     )
     n_d, n_h = attn_gain.shape[0], q_gain.shape[0]
-    block_rows, grad_proj, ffn_sums, grad_res, attn_sums, down_sum, gu_grad = middle_call(
+    block_rows, grad_proj, ffn_sums, grad_res, attn_sums, down_sum, gu_grad, down_in, gate_sum = middle_call(
         nb, res_all, w_mlp, res_mine, out_grad, proj_mine, inv_mine, width_gain
     )
     grad_rows, sums, down_grad, gu_grad, qkv_grad, out_grad_w = last_call(
@@ -1326,6 +1410,8 @@
         ffn_sums,
         down_sum,
         gu_grad,
+        down_in,
+        gate_sum,
     )
     width_sums = lax.dynamic_slice_in_dim(sums[:2, :quarter], b * n_d, n_d, 1)
     head_sums = lax.dynamic_slice_in_dim(sums[:2, quarter:], b * n_h, n_h, 1)

time: 440 us -> 435 us (0.989)
  Pallas kernels: 422 us -> 415 us
    pallas_call x1, Pallas kernels: 130 us -> 107 us  [last_call(): pl.pallas_call(functools.partial(last_kernel, na, nb), out_shape=outs, in...]
    pallas_call x1, Pallas kernels: 135 us -> 151 us  [middle_call(): pl.pallas_call(functools.partial(middle_kernel, na, nb), out_shape=outs,...]
where the time goes in v2:
time: 435 us; the launch traced here: 433 us
  Pallas kernels  415 us (95%)
  local copies, waits for them, and re-layouts  10.6 us (2%)
  other arithmetic  6.57 us (2%)
    pallas_call x1, Pallas kernels, enter_call(): pl.pallas_call(functools.partial(enter_kernel, na, nb, sizes), out_shape=...  157 us
    pallas_call x1, Pallas kernels, middle_call(): pl.pallas_call(functools.partial(middle_kernel, na, nb), out_shape=outs,...  151 us
    pallas_call x1, Pallas kernels, last_call(): pl.pallas_call(functools.partial(last_kernel, na, nb), out_shape=outs, in...  107 us

profile of v2, /device:TPU:8, one launch (start us, length us, event | category | flops | bytes accessed | tf_op | source)
XLA Modules:
  0.0 432.8 jit_solution(5933402112587461812)
XLA Ops:
  0.7 0.5 fusion
  1.2 0.8 pad_maximum_fusion
  2.0 0.8 pad_maximum_fusion.2
  2.8 0.6 broadcast_in_dim.2.refs_7_
  3.4 156.7 %enter.1 = (bf16[4,256,2048]{2,1,0:T(8,128)(2,1)}, bf16[2048,512]{1,0:T(8,128)(2,1)}, bf16[2048,1536]{1,0:T(8,128)(2,1)}, f32[8,512]{1,0:T(8,128)}, f32[8,128]{1...) custom-call(bf16[256,2048]{1,0:T(8,128)(2,1)} %refs_0_.1, ...), custom_call_target="tpu_custom_call" | custom-call | tf_op jit(solution)/shard_map/enter/pallas_call | solution.py:1307
  160.1 151.0 %middle.1 = (bf16[1,256,2048]{2,1,0:T(8,128)(2,1)}, bf16[4,256,2048]{2,1,0:T(8,128)(2,1)}, f32[8,512]{1,0:T(8,128)}, f32[256,512]{1,0:T(8,128)}, f32[8,512]{1,0:...) custom-call(bf16[4,256,2048]{2,1,0:T(8,128)(2,1)} %get-tuple-element, ...), custom_call_target="tpu_custom_call" | custom-call | tf_op jit(solution)/shard_map/middle/pallas_call | solution.py:725
  311.1 107.2 %last.1 = (bf16[1,256,2048]{2,1,0:T(8,128)(2,1)}, f32[8,640]{1,0:T(8,128)}, f32[256,2048]{1,0:T(8,128)}, f32[256,2,2048]{2,1,0:T(2,128)}, f32[3,256,512]{2,1,0:T(8,128)}, /*index=5*/f32[256,512]{1,0:T(8,128)}) custom-call(bf16[4,256,2048]{2,1,0:T(8,128)(2,1)} %get-tuple-element.44.refs_0_, bf16[4,256,2048]{2,1,0:T(8,128)(2,1)} %get-tuple-element.45.refs_1_, ...), custom_call_target="tpu_custom_call" | custom-call | tf_op jit(solution)/shard_map/last/pallas_call | solution.py:1004
  418.3 0.0 copy-start.3
  418.4 2.9 bitcast_convert_fusion
  421.2 0.8 slice.18
  422.1 0.6 fusion.2
  422.7 0.7 slice.21
  423.4 0.1 constant_dynamic-slice_fusion.1
  423.5 0.5 slice_bitcast_fusion
  424.0 0.0 copy-done.3
  424.0 1.6 bitcast_convert_fusion.1
  425.5 0.0 copy-done.2
  425.6 1.1 copy.24
  426.7 0.9 copy-done.4
  427.6 0.8 copy.25
  428.4 0.0 copy-done
  428.4 2.1 copy.26
  430.5 1.0 copy-done.1
  431.5 1.3 copy.27
  (5 shorter events, 0.0 us)
Async XLA Ops:
  418.3 5.6 %copy-start.3 = (bf16[1,256,2048]{2,1,0:T(8,128)(2,1)S(1)}, bf16[1,256,2048]{2,1,0:T(8,128)(2,1)}, u32[]{:S(2)}) copy-start(bf16[1,256,2048]{2,1,0:T(8,128)(2,1)} %get-tuple-element.43) | copy-start | bytes 3145732
  421.2 4.3 copy-start.2
  424.0 4.4 %copy-start = (f32[256,2,2048]{2,1,0:T(2,128)S(1)}, f32[256,2,2048]{2,1,0:T(2,128)}, u32[]{:S(2)}) copy-start(f32[256,2,2048]{2,1,0:T(2,128)} %get-tuple-element.86) | copy-start | bytes 12582916
  425.5 2.1 copy-start.4
  428.4 3.1 copy-start.1

commit v3 on v2

--- a/solution.py
+++ b/solution.py
@@ -556,18 +556,30 @@
 
 
 def middle_kernel(na, nb, *refs):
-    x_ref, w_ref, res_ref, grad_far, proj_ref, inv_ref, gain_ref = refs[:7]
-    block_ref, back_out, ffn_sum_ref, grad_res_ref, attn_sum_ref, down_sum_ref, gu_grad_ref = refs[7:14]
+    x_far, w_far, res_ref, grad_far, proj_ref, inv_ref, gain_ref = refs[:7]
+    block_ref, back_out, ffn_sum_ref, grad_res_ref, attn_sum_ref, down_sum_ref, up_grad_far = refs[7:14]
     down_in, gate_sum_ref = refs[14:16]
     out, hidden_ref, grad_gu_ref, gu_ref, part_ref, down_grad, down_held, grad_ref, gu_held = refs[16:25]
-    scratch, (local_sem, send_sem, recv_sem) = refs[25:-3], refs[-3:]
+    x_ref, w_ref, gu_grad_ref = refs[25:28]
+    scratch, (local_sem, send_sem, recv_sem) = refs[28:-3], refs[-3:]
     share = 2 * lax.axis_index("q") + lax.axis_index("p")
     load = pltpu.make_async_copy(
         grad_far.at[:, span(share, grad_ref.shape[1])], grad_ref, local_sem.at[0]
     )
     load.start()
+    load_w = pltpu.make_async_copy(w_far, w_ref, local_sem.at[1])
+    load_w.start()
+    load_x = {
+        k: pltpu.make_async_copy(x_far.at[k], x_ref.at[k], local_sem.at[2 + k])
+        for k in list(range(2, na)) + [1, 0]
+    }
+    for copy in load_x.values():
+        copy.start()
     units = hidden_ref.shape[2]
     width = x_ref.shape[2]
+    save_up = pltpu.make_async_copy(
+        gu_grad_ref.at[:, :, :, units:], up_grad_far, local_sem.at[2 + na]
+    )
     b = lax.axis_index("b")
     greet(reduce_peers(na) + [{"b": across(b, j)} for j in range(1, nb)])
     links = Links(send_sem, recv_sem)
@@ -627,13 +639,17 @@
     back_first, back_second = back_math(
         s, grad_ref, proj_ref, inv_ref, gain_ref, grad_res_ref, attn_sum_ref
     )
-    copies, reused = {}, []
+    copies, reused, loaded, blocks = {}, [], [], []
     gate = slice(0, units)
 
     def half(c):
         return slice(c * units // 2, (c + 1) * units // 2)
 
     def forward_step(k):
+        if not loaded:
+            load_w.wait()
+        loaded.append(k)
+        load_x[k].wait()
         forward(k)
         for h in range(HALVES):
             r.send_q(h, k)
@@ -671,6 +687,12 @@
         copies["z", c, k] = links.send(
             down_sum_ref.at[across(r.a, k), :, half(c)], down_in.at[k - 1, :, half(c)], {"a": across(r.a, k)}
         )
+
+    def gu_grads(block):
+        weight_grad(x_ref, grad_gu_ref, gu_grad_ref, block)
+        blocks.append(block)
+        if len(blocks) == na:
+            save_up.start()
 
     def gate_rows():
         copies["g"] = exchange_b(links, gu_grad_ref, gu_held, gate)
@@ -687,7 +709,7 @@
         "SG": lambda: sum_b(
             copies["g"], lambda block: gu_grad_ref.at[block, b], gu_held, gate_sum_ref, gate
         ),
-        "G": lambda block: weight_grad(x_ref, grad_gu_ref, gu_grad_ref, block),
+        "G": gu_grads,
     }
     table.update({"r" + key: step for key, step in r.steps(first, second, 2).items()})
     table.update({"s" + key: step for key, step in s.steps(back_first, back_second, 1).items()})
@@ -701,6 +723,7 @@
     for c in range(2):
         for k in range(1, na):
             copies["z", c, k].wait_recv()
+    save_up.wait()
     links.finish()
 
 
@@ -717,7 +740,7 @@
         shape((rows, quarter), f32),
         shape((8, quarter), f32),
         shape((na, w_rows, units), bf16),
-        shape((na, nb, w_rows, 2 * units), bf16),
+        shape((na, nb, w_rows, units), bf16),
         shape((na - 1, w_rows, units), bf16),
         shape((na, w_rows, units), bf16),
     )
@@ -725,8 +748,8 @@
     return pl.pallas_call(
         functools.partial(middle_kernel, na, nb),
         out_shape=outs,
-        in_specs=[far if i == 3 else vmem for i in range(7)],
-        out_specs=(vmem,) * len(outs),
+        in_specs=[far if i in (0, 1, 3) else vmem for i in range(7)],
+        out_specs=tuple(far if i == 6 else vmem for i in range(len(outs))),
         scratch_shapes=[
             pltpu.VMEM((na, rows, width), bf16),
             pltpu.VMEM((na, rows, units), bf16),
@@ -737,11 +760,14 @@
             pltpu.VMEM((nb - 1, na, w_rows, units), bf16),
             pltpu.VMEM((rows, quarter), f32),
             pltpu.VMEM((nb - 1, na, w_rows, units), bf16),
+            pltpu.VMEM((na, rows, width), bf16),
+            pltpu.VMEM((width, 3 * units), bf16),
+            pltpu.VMEM((na, nb, w_rows, 2 * units), bf16),
         ]
         + reduce_scratch(na, rows, width)
         + reduce_scratch(na, rows, width)
         + [
-            pltpu.SemaphoreType.DMA((1,)),
+            pltpu.SemaphoreType.DMA((3 + na,)),
             pltpu.SemaphoreType.DMA((copies,)),
             pltpu.SemaphoreType.DMA((copies,)),
         ],
@@ -767,20 +793,32 @@
 
 
 def last_kernel(na, nb, *refs):
-    proj_ref, x_far, qkv_ref, stats_ref, gain_ref, cos_ref, sin_ref, w_ref, att_ref = refs[:9]
-    grad_ref, attn_sum_ref, ffn_sum_ref, down_sum_ref, gu_grad_far, down_in, gate_ref = refs[9:16]
+    proj_far, x_far, qkv_ref, stats_ref, gain_ref, cos_ref, sin_ref, w_ref, att_ref = refs[:9]
+    grad_ref, attn_sum_ref, ffn_sum_ref, down_sum_far, up_grad_far, down_in_far, gate_ref = refs[9:16]
     out, sums_ref, down_far, gu_far, qkv_out, wout_out = refs[16:22]
     scaled_ref, grad_qkv_ref, part_ref, head_sums, held, stats_a, inner_ref = refs[22:29]
     own_sums, a_sums, b_sums, up_held, up_sum, attn_grad, attn_held, attn_sum = refs[29:37]
     gu_in, attn_in, x_ref, up_own, down_out, gu_out = refs[37:43]
-    scratch, (local_sem, send_sem, recv_sem) = refs[43:-3], refs[-3:]
+    proj_ref, down_sum_ref, down_in = refs[43:46]
+    scratch, (local_sem, send_sem, recv_sem) = refs[46:-3], refs[-3:]
+    load_proj = [
+        pltpu.make_async_copy(proj_far.at[k], proj_ref.at[k], local_sem.at[4 + k]) for k in range(na)
+    ]
+    for copy in load_proj:
+        copy.start()
     links = Links(send_sem, recv_sem)
     load_gu = pltpu.make_async_copy(
-        gu_grad_far.at[:, lax.axis_index("b"), :, gate_ref.shape[2] :], up_own, local_sem.at[0]
+        up_grad_far.at[:, lax.axis_index("b")], up_own, local_sem.at[0]
     )
     load_gu.start()
     load_x = pltpu.make_async_copy(x_far, x_ref, local_sem.at[1])
     load_x.start()
+    load_down = [
+        pltpu.make_async_copy(down_sum_far, down_sum_ref, local_sem.at[4 + na]),
+        pltpu.make_async_copy(down_in_far, down_in, local_sem.at[5 + na]),
+    ]
+    for copy in load_down:
+        copy.start()
     save_down = pltpu.make_async_copy(down_out, down_far, local_sem.at[2])
     save_gu = pltpu.make_async_copy(gu_out, gu_far, local_sem.at[3])
     r = Reduce(na, links, part_ref, out, scratch)
@@ -795,7 +833,7 @@
     head_sums[...] = jnp.zeros_like(head_sums)
     greet(reduce_peers(na) + [{"b": across(b, j)} for j in range(1, nb)])
     copies, stored = {}, []
-    whole, upper = slice(0, units), slice(units, 2 * units)
+    whole = slice(0, units)
     attn_columns = slice(0, 4 * HD)
     over_heads = OverHeads(links, na, a, p, q, held, stats_a, inner_ref)
 
@@ -837,9 +875,20 @@
             total = total + b_sums[j]
         sums_ref[...] = total
 
+    def proj_here(k):
+        if ("proj", k) not in copies:
+            copies["proj", k] = True
+            load_proj[k].wait()
+
+    def out_grads(block):
+        for k in range(na):
+            proj_here(k)
+        weight_grad(proj_ref, att_ref, attn_grad, block, slice(3 * HD, 4 * HD))
+
     def attend_back(k):
-        if k % 2 == 0:
-            lax.fori_loop(k, k + 2, attend_back_block, 0)
+        proj_here(k)
+        if k % 2:
+            lax.fori_loop(k - 1, k + 1, attend_back_block, 0)
 
     def attend_back_block(k, carry):
         queries, key_rows, values, q_inv, k_inv, q_rot, k_rot, probs = attention(
@@ -889,7 +938,7 @@
         weight_grad(x_ref, grad_qkv_ref, attn_grad, block, slice(0, 3 * HD))
 
     def up_rows(_):
-        copies["up"] = exchange_b(links, gu_grad_far, up_held, upper)
+        copies["up"] = exchange_b(links, up_grad_far, up_held, whole)
 
     def up_sums(_):
         load_gu.wait()
@@ -941,6 +990,8 @@
     def down_rows(k):
         if "down" not in copies:
             copies["down"] = 0
+            for copy in load_down:
+                copy.wait()
             store(down_out, a, units, down_sum_ref[a])
         store(down_out, across(a, k), units, down_in[k - 1])
         copies["down"] += 1
@@ -961,7 +1012,7 @@
         "S2": over_heads.to_core,
         "S3": over_heads.to_all,
         "S4": over_heads.done,
-        "WO": lambda block: weight_grad(proj_ref, att_ref, attn_grad, block, slice(3 * HD, 4 * HD)),
+        "WO": out_grads,
         "WQ": qkv_grads,
         "QB": qkv_back,
         "YG": up_rows,
@@ -1004,7 +1055,7 @@
     return pl.pallas_call(
         functools.partial(last_kernel, na, nb),
         out_shape=outs,
-        in_specs=[far if i in (1, 13) else vmem for i in range(16)],
+        in_specs=[far if i in (0, 1, 12, 13, 14) else vmem for i in range(16)],
         out_specs=(vmem, vmem, far, far, vmem, vmem),
         scratch_shapes=[
             pltpu.VMEM((na, rows, 2 * HD), f32),
@@ -1028,10 +1079,13 @@
             pltpu.VMEM((na, w_rows, units), bf16),
             pltpu.VMEM((w_rows, na * units), f32),
             pltpu.VMEM((w_rows, 2, na * units), f32),
+            pltpu.VMEM((na, rows, width), bf16),
+            pltpu.VMEM((na, w_rows, units), bf16),
+            pltpu.VMEM((na - 1, w_rows, units), bf16),
         ]
         + reduce_scratch(na, rows, width)
         + [
-            pltpu.SemaphoreType.DMA((4,)),
+            pltpu.SemaphoreType.DMA((6 + na,)),
             pltpu.SemaphoreType.DMA((copies,)),
             pltpu.SemaphoreType.DMA((copies,)),
         ],
@@ -1075,13 +1129,19 @@
 
 
 def enter_kernel(na, nb, gain_sizes, *refs):
-    tok_far, qkv_w_ref, wout_ref, gu_ref, down_ref, cos_ref, sin_ref, all_gains_ref = refs[:8]
+    tok_far, qkv_w_ref, wout_ref, gu_far, down_far, cos_ref, sin_ref, all_gains_ref = refs[:8]
     x_far, w_far, mlp_w_ref, width_gain_ref, head_gain_ref, qkv_far, stats_ref, att_far = refs[8:16]
     out, proj_ref, inv_ref, res_ref = refs[16:20]
     own_gains, gains_ref, piece_ref, part_ref, held, stats_a = refs[20:26]
     x_ref, w_ref, qkv_ref, att_ref = refs[26:30]
-    tok_ref = refs[30]
-    scratch, (local_sem, send_sem, recv_sem) = refs[31:-3], refs[-3:]
+    tok_ref, gu_ref, down_ref = refs[30:33]
+    scratch, (local_sem, send_sem, recv_sem) = refs[33:-3], refs[-3:]
+    load_mlp = [
+        pltpu.make_async_copy(gu_far, gu_ref, local_sem.at[10]),
+        pltpu.make_async_copy(down_far, down_ref, local_sem.at[11]),
+    ]
+    for copy in load_mlp:
+        copy.start()
     saves = [
         pltpu.make_async_copy(near, there, local_sem.at[5 + i])
         for i, (near, there) in enumerate(
@@ -1163,6 +1223,10 @@
         copies["x", k] = links.send(at, at, {"q": 1 - q})
 
     def cut_weights(k):
+        if "cut" not in copies:
+            copies["cut"] = True
+            for copy in load_mlp:
+                copy.wait()
         block = span(across(a, k), units)
 
         def cut(i, carry):
@@ -1307,7 +1371,7 @@
     return pl.pallas_call(
         functools.partial(enter_kernel, na, nb, sizes),
         out_shape=tuple(outs),
-        in_specs=[far] + [vmem] * 7,
+        in_specs=[far if i in (0, 3, 4) else vmem for i in range(8)],
         out_specs=tuple(far if i in (0, 1, 5, 7) else vmem for i in range(len(outs))),
         scratch_shapes=[
             pltpu.VMEM((8, lanes), f32),
@@ -1321,10 +1385,12 @@
             pltpu.VMEM((na, rows, 3 * HD), f32),
             pltpu.VMEM((na, rows, HD), bf16),
             pltpu.VMEM((rows, quarter), bf16),
+            pltpu.VMEM(gu.shape, bf16),
+            pltpu.VMEM(down.shape, bf16),
         ]
         + reduce_scratch(na, rows, width)
         + [
-            pltpu.SemaphoreType.DMA((10,)),
+            pltpu.SemaphoreType.DMA((12,)),
             pltpu.SemaphoreType.DMA((copies,)),
             pltpu.SemaphoreType.DMA((copies,)),
         ],

time: 435 us -> 429 us (0.986)
  Pallas kernels: 415 us -> 409 us
    pallas_call x1, Pallas kernels: 151 us -> 147 us  [middle_call(): pl.pallas_call(functools.partial(middle_kernel, na, nb), out_shape=outs,...]
where the time goes in v3:
time: 429 us; the launch traced here: 427 us
  Pallas kernels  409 us (95%)
  local copies, waits for them, and re-layouts  10.6 us (2%)
  other arithmetic  6.57 us (2%)
    pallas_call x1, Pallas kernels, enter_call(): pl.pallas_call(functools.partial(enter_kernel, na, nb, sizes), out_shape=...  156 us
    pallas_call x1, Pallas kernels, middle_call(): pl.pallas_call(functools.partial(middle_kernel, na, nb), out_shape=outs,...  147 us
    pallas_call x1, Pallas kernels, last_call(): pl.pallas_call(functools.partial(last_kernel, na, nb), out_shape=outs, in...  107 us

profile of v3, /device:TPU:8, one launch (start us, length us, event | category | flops | bytes accessed | tf_op | source)
XLA Modules:
  0.0 427.1 jit_solution(11608072861830144173)
XLA Ops:
  0.7 0.5 fusion
  1.2 0.8 pad_maximum_fusion
  2.0 0.8 pad_maximum_fusion.2
  2.8 0.6 broadcast_in_dim.2.refs_7_
  3.4 156.0 %enter.1 = (bf16[4,256,2048]{2,1,0:T(8,128)(2,1)}, bf16[2048,512]{1,0:T(8,128)(2,1)}, bf16[2048,1536]{1,0:T(8,128)(2,1)}, f32[8,512]{1,0:T(8,128)}, f32[8,128]{1...) custom-call(bf16[256,2048]{1,0:T(8,128)(2,1)} %refs_0_.1, ...), custom_call_target="tpu_custom_call" | custom-call | tf_op jit(solution)/shard_map/enter/pallas_call | solution.py:1371
  159.4 146.6 %middle.1 = (bf16[1,256,2048]{2,1,0:T(8,128)(2,1)}, bf16[4,256,2048]{2,1,0:T(8,128)(2,1)}, f32[8,512]{1,0:T(8,128)}, f32[256,512]{1,0:T(8,128)}, f32[8,512]{1,0:...) custom-call(bf16[4,256,2048]{2,1,0:T(8,128)(2,1)} %get-tuple-element, ...), custom_call_target="tpu_custom_call" | custom-call | tf_op jit(solution)/shard_map/middle/pallas_call | solution.py:748
  306.1 106.5 %last.1 = (bf16[1,256,2048]{2,1,0:T(8,128)(2,1)}, f32[8,640]{1,0:T(8,128)}, f32[256,2048]{1,0:T(8,128)}, f32[256,2,2048]{2,1,0:T(2,128)}, f32[3,256,512]{2,1,0:T(8,128)}, /*index=5*/f32[256,512]{1,0:T(8,128)}) custom-call(bf16[4,256,2048]{2,1,0:T(8,128)(2,1)} %get-tuple-element.44.refs_0_, bf16[4,256,2048]{2,1,0:T(8,128)(2,1)} %get-tuple-element.45.refs_1_, ...), custom_call_target="tpu_custom_call" | custom-call | tf_op jit(solution)/shard_map/last/pallas_call | solution.py:1055
  412.6 0.0 copy-start.3
  412.6 2.9 bitcast_convert_fusion
  415.5 0.8 slice.18
  416.3 0.6 fusion.2
  417.0 0.7 slice.21
  417.7 0.1 constant_dynamic-slice_fusion.1
  417.7 0.5 slice_bitcast_fusion
  418.3 0.0 copy-done.3
  418.3 1.6 bitcast_convert_fusion.1
  419.8 0.0 copy-done.2
  419.8 1.1 copy.24
  421.0 0.9 copy-done.4
  421.9 0.8 copy.25
  422.7 0.0 copy-done
  422.7 2.1 copy.26
  424.8 1.0 copy-done.1
  425.8 1.3 copy.27
  (5 shorter events, 0.0 us)
Async XLA Ops:
  412.6 5.6 %copy-start.3 = (bf16[1,256,2048]{2,1,0:T(8,128)(2,1)S(1)}, bf16[1,256,2048]{2,1,0:T(8,128)(2,1)}, u32[]{:S(2)}) copy-start(bf16[1,256,2048]{2,1,0:T(8,128)(2,1)} %get-tuple-element.43) | copy-start | bytes 3145732
  415.5 4.3 %copy-start.2 = (f32[3,256,512]{2,1,0:T(8,128)S(1)}, f32[3,256,512]{2,1,0:T(8,128)}, u32[]{:S(2)}) copy-start(f32[3,256,512]{2,1,0:T(8,128)} %get-tuple-element.59) | copy-start | bytes 4718596
  418.3 4.4 %copy-start = (f32[256,2,2048]{2,1,0:T(2,128)S(1)}, f32[256,2,2048]{2,1,0:T(2,128)}, u32[]{:S(2)}) copy-start(f32[256,2,2048]{2,1,0:T(2,128)} %get-tuple-element.86) | copy-start | bytes 12582916
  419.8 2.1 copy-start.4
  422.7 3.1 copy-start.1

commit v4 on v3

--- a/solution.py
+++ b/solution.py
@@ -283,7 +283,7 @@
         self.lead = list(range(2, na)) + [1, 0]
         self.step_q, self.step_p, self.step_a = {}, {}, {}
         self.spread_a, self.spread_p, self.spread_q, self.stats = {}, {}, {}, {}
-        self.here = set()
+        self.here, self.slots = set(), None
 
     def at(self, h):
         return slice(h * self.count, (h + 1) * self.count)
@@ -328,6 +328,8 @@
         )
 
     def add_all(self, at):
+        if self.slots is not None:
+            return self.total[at]
         own = self.half_sum[0, at, span(self.p, self.quarter)].astype(f32)
         own = own + self.from_p[0, at].astype(f32)
         for k in range(1, self.na):
@@ -335,9 +337,12 @@
         return own
 
     def scattered(self, h, first, number):
-        self.step_p[h, 0].wait_recv()
-        for k in range(1, self.na):
-            self.step_a[h, k].wait_recv()
+        if self.slots is not None:
+            self.gather_sums(h)
+        else:
+            self.step_p[h, 0].wait_recv()
+            for k in range(1, self.na):
+                self.step_a[h, k].wait_recv()
         self.each(h, first)
         if number:
             at = self.at(h)
@@ -385,6 +390,98 @@
         if (h, k) not in self.here:
             self.here.add((h, k))
             self.spread_q[h, k].wait_recv()
+
+    def chained(self, slots):
+        self.slots = slots
+        na = self.na
+        self.base_p = [self.links.reserve(na) for _ in range(HALVES)]
+        self.base_c = [{w: self.links.reserve(na - 1) for w in (1, -1)} for _ in range(HALVES)]
+        self.links.lines.append(self)
+
+    def copy_p(self, h, k):
+        at = self.at(h)
+        source = self.half_sum.at[k, at, span(1 - self.p, self.quarter)]
+        return self.links.copy(self.base_p[h] + k, source, self.from_p.at[k, at], {"p": 1 - self.p})
+
+    def copy_c(self, h, way, t):
+        at, side = self.at(h), 0 if way == 1 else 1
+        return self.links.copy(
+            self.base_c[h][way] + t - 1,
+            self.slots.at[0, side, t - 1, at],
+            self.slots.at[1, side, t - 1, at],
+            {"a": (self.a + way) % self.na},
+        )
+
+    def inside(self, index):
+        return (index >= 0) & (index < self.na)
+
+    def send_p_chained(self, h, k):
+        self.step_q[h, k].wait_recv()
+
+        def add(at):
+            own = self.part[k, at, span(self.q, self.half)].astype(f32)
+            self.half_sum[k, at] = (own + self.from_q[k, at].astype(f32)).astype(bf16)
+
+        self.each(h, add)
+        self.copy_p(h, k).start()
+
+    def pass_sums(self, h, way, t):
+        side = 0 if way == 1 else 1
+
+        @pl.when(self.inside(self.a + way * t))
+        def _():
+            k = exclusive_or(self.a, self.a + way * t, self.na)
+            self.copy_p(h, k).wait_recv()
+
+            def add(at):
+                own = self.half_sum[k, at, span(self.p, self.quarter)].astype(f32)
+                self.slots[0, side, t - 1, at] = (own + self.from_p[k, at].astype(f32)).astype(bf16)
+
+            self.each(h, add)
+            if t < self.na - 1:
+
+                @pl.when(self.inside(self.a - way))
+                def _():
+                    self.copy_c(h, way, t + 1).wait_recv()
+
+                    def more(at):
+                        own = self.slots[0, side, t - 1, at].astype(f32)
+                        came = self.slots[1, side, t, at].astype(f32)
+                        self.slots[0, side, t - 1, at] = (own + came).astype(bf16)
+
+                    self.each(h, more)
+
+            self.copy_c(h, way, t).start()
+
+    def gather_sums(self, h):
+        self.copy_p(h, 0).wait_recv()
+
+        def own(at):
+            here = self.half_sum[0, at, span(self.p, self.quarter)].astype(f32)
+            self.total[at] = here + self.from_p[0, at].astype(f32)
+
+        self.each(h, own)
+        for side, way in enumerate((1, -1)):
+
+            @pl.when(self.inside(self.a - way))
+            def _(side=side, way=way):
+                self.copy_c(h, way, 1).wait_recv()
+
+                def more(at):
+                    self.total[at] += self.slots[1, side, 0, at].astype(f32)
+
+                self.each(h, more)
+
+    def finish(self):
+        for h in range(HALVES):
+            for k in range(self.na):
+                self.copy_p(h, k).wait_send()
+            for way in (1, -1):
+                for t in range(1, self.na):
+
+                    @pl.when(self.inside(self.a + way * t))
+                    def _(h=h, way=way, t=t):
+                        self.copy_c(h, way, t).wait_send()
 
     def steps(self, first, second, number, chain=False):
         def normed(h):
@@ -411,6 +508,12 @@
             "RP": self.relay_p,
             "RQ": self.relay_q,
         }
+        if self.slots is not None:
+            table.update(
+                P=self.send_p_chained,
+                CR=lambda h, t: self.pass_sums(h, 1, t),
+                CL=lambda h, t: self.pass_sums(h, -1, t),
+            )
         if chain:
             lines = [
                 Line(
@@ -779,16 +882,16 @@
 
 
 LAST = (
-    ("ZG", 0, 2), ("U1",), ("YG", 1), ("AB", 0), ("U2",), ("AB", 1), ("ZG", 0, 1), ("AB", 2),
-    ("WO", 3), ("U3",), ("ZG", 0, 3), ("AB", 3), ("OD", 2), ("S1",), ("S2",), ("S3",), ("WO", 0),
-    ("SG", 1), ("ZG", 1, 2), ("S4",), ("QB", 1), ("QB", 0), ("QB", 2), ("QB", 3), ("U4",), ("OWNG",),
-    ("OG", 0, 3), ("WQ", 1), ("ZG", 1, 3), ("rP", 1, 3), ("WQ", 2), ("rP", 0, 0), ("ZG", 1, 1),
-    ("OG", 0, 1), ("rP", 1, 2), ("rP", 0, 1), ("WQ", 0), ("rP", 1, 0), ("WO", 1), ("rA", 1, 3),
-    ("WO", 2), ("WQ", 3), ("YA",), ("OG", 0, 2), ("OD", 1), ("rP", 0, 2), ("rA", 1, 2), ("rA", 0, 1),
-    ("OG", 1, 1), ("OG", 1, 2), ("rA", 0, 2), ("rP", 1, 1), ("rP", 0, 3), ("rA", 1, 1), ("OD", 3),
-    ("rA", 0, 3), ("OG", 1, 3), ("rSC", 1), ("SA",), ("ZA", 2), ("U5",), ("rSC", 0), ("rX", 0), ("ZA", 3),
-    ("ZA", 1), ("OWN",), ("rX", 1), ("rRQ", 0, 0), ("OA", 2), ("OA", 1), ("rRQ", 1, 0),
-    ("OA", 3),
+    ("U1",), ("ZG", 0, 3), ("YG", 1), ("AB", 0), ("AB", 1), ("U2",), ("AB", 2), ("AB", 3),
+    ("S1",), ("WO", 1), ("U3",), ("S2",), ("WO", 2), ("S3",), ("ZG", 0, 1), ("ZG", 0, 2), ("WO", 3),
+    ("WO", 0), ("OG", 0, 3), ("S4",), ("QB", 3), ("OD", 2), ("QB", 2), ("QB", 0), ("SG", 1), ("rP", 1, 3),
+    ("ZG", 1, 2), ("QB", 1), ("ZG", 1, 3), ("rP", 1, 0), ("rP", 0, 0), ("WQ", 1), ("rP", 1, 2),
+    ("WQ", 2), ("WQ", 0), ("rP", 0, 2), ("OD", 1), ("rP", 0, 3), ("WQ", 3), ("ZG", 1, 1),
+    ("YA",), ("rP", 1, 1), ("rP", 0, 1), ("OG", 0, 1), ("rCL", 1, 3), ("rCR", 0, 3),
+    ("rCR", 1, 3), ("OG", 0, 2), ("OD", 3), ("rCL", 0, 3), ("rCR", 0, 2), ("rCR", 1, 2), ("rCL", 1, 2),
+    ("rCL", 0, 2), ("OG", 1, 1), ("OG", 1, 2), ("rCR", 0, 1), ("rCL", 1, 1), ("rCR", 1, 1), ("rCL", 0, 1),
+    ("SA",), ("ZA", 2), ("OG", 1, 3), ("ZA", 1), ("rSC", 0), ("ZA", 3), ("rSC", 1), ("rX", 0), ("U4",), ("OWNG",),
+    ("OA", 2), ("rX", 1), ("U5",), ("OWN",), ("rRQ", 0, 0), ("rRQ", 1, 0), ("OA", 1), ("OA", 3),
 )
 
 
@@ -822,6 +925,7 @@
     save_down = pltpu.make_async_copy(down_out, down_far, local_sem.at[2])
     save_gu = pltpu.make_async_copy(gu_out, gu_far, local_sem.at[3])
     r = Reduce(na, links, part_ref, out, scratch)
+    r.chained(scratch[9])
     a, b, p, q, mine, pair, quarter = (
         r.a, lax.axis_index("b"), r.p, r.q, r.mine, r.pair, r.quarter,
     )
@@ -1051,7 +1155,7 @@
         shape((3, w_rows, na * HD), f32),
         shape((w_rows, na * HD), f32),
     )
-    copies = HALVES * (3 * na + 1) + 2 + 6 * na + 4 * nb
+    copies = HALVES * (6 * na + 1) + 2 + 6 * na + 4 * nb
     return pl.pallas_call(
         functools.partial(last_kernel, na, nb),
         out_shape=outs,
@@ -1083,7 +1187,7 @@
             pltpu.VMEM((na, w_rows, units), bf16),
             pltpu.VMEM((na - 1, w_rows, units), bf16),
         ]
-        + reduce_scratch(na, rows, width)
+        + reduce_scratch(na, rows, width, True)
         + [
             pltpu.SemaphoreType.DMA((6 + na,)),
             pltpu.SemaphoreType.DMA((copies,)),
@@ -1096,8 +1200,9 @@
     )(*operands)
 
 
-def reduce_scratch(na, rows, width):
+def reduce_scratch(na, rows, width, chained=False):
     quarter = width // 4
+    slots = [pltpu.VMEM((2, 2, na - 1, rows, quarter), bf16)] if chained else []
     return [
         pltpu.VMEM((na, rows, width // 2), bf16),
         pltpu.VMEM((na, rows, width // 2), bf16),
@@ -1108,23 +1213,24 @@
         pltpu.VMEM((2, rows, 128), f32),
         pltpu.VMEM((2, rows, 128), f32),
         pltpu.VMEM((HALVES, 4, 8, rows // HALVES), f32),
-    ]
+    ] + slots
 
 
 ENTER = (
-    ("Z", 0), ("W", 3), ("FW", 0), ("FR", 0, 1), ("FL", 0, 1), ("W", 1), ("CUT", 2), ("FW", 1), ("W", 2),
-    ("FR", 0, 2), ("FR", 0, 3), ("CUT", 3), ("M", 0, 3), ("FL", 0, 2), ("CUT", 1), ("FW", 3), ("FL", 0, 3),
-    ("GA",), ("FT", 0), ("FQ", 3), ("FW", 2), ("CUT", 0), ("FQ", 2), ("M", 0, 1), ("M", 2, 3), ("FQ", 1),
-    ("J", 3), ("FQ", 0), ("J", 0), ("GB",), ("M", 1, 1), ("J", 1), ("J", 2), ("S1",), ("S2",), ("S3",),
-    ("M", 1, 3), ("MR", 1, 0), ("M", 1, 2), ("S4",), ("E", 3), ("E", 1), ("rP", 1, 3), ("E", 2),
-    ("rP", 1, 1), ("M", 2, 1), ("MR", 2, 3), ("rP", 0, 3), ("rP", 0, 1), ("MR", 0, 3), ("E", 0),
-    ("rA", 1, 3), ("MR", 2, 0), ("rA", 1, 1), ("MR", 0, 1), ("rA", 0, 3), ("MR", 1, 3), ("rP", 0, 2),
-    ("MR", 2, 1), ("rA", 0, 2), ("rA", 0, 1), ("rP", 0, 0), ("rP", 1, 2), ("rA", 1, 2), ("MR", 1, 2),
-    ("rP", 1, 0), ("rSC", 0), ("rSQ", 0), ("MR", 0, 0), ("M", 2, 2), ("rSC", 1), ("rSD", 0), ("rSQ", 1),
-    ("rX", 0), ("rSD", 1), ("rZ", 0), ("rZ", 1), ("rFR", 0, 1), ("rFL", 0, 1), ("rX", 1), ("MR", 2, 2),
-    ("rFR", 1, 1), ("rFL", 1, 1), ("rFR", 0, 2), ("rRQ", 0, 0), ("rFL", 1, 2), ("rFL", 0, 2), ("MR", 1, 1),
-    ("rFR", 0, 3), ("M", 0, 2), ("rFR", 1, 2), ("rFL", 1, 3), ("rFR", 1, 3), ("rFL", 0, 3), ("rRQ", 0, 1),
-    ("MR", 0, 2), ("rRQ", 1, 1), ("rRQ", 1, 2), ("rRQ", 0, 2), ("rRQ", 1, 0), ("rRQ", 1, 3), ("rRQ", 0, 3),
+    ("Z", 0), ("W", 3), ("FL", 0, 1), ("FR", 0, 1), ("W", 1), ("GA",), ("CUT", 0), ("FW", 0), ("FT", 0),
+    ("CUT", 3), ("FW", 1), ("W", 2), ("CUT", 1), ("M", 0, 1), ("FL", 0, 2), ("FW", 3), ("CUT", 2),
+    ("FW", 2), ("FL", 0, 3), ("FR", 0, 2), ("FQ", 0), ("FR", 0, 3), ("M", 0, 3), ("FQ", 2), ("M", 1, 2),
+    ("M", 2, 1), ("J", 2), ("FQ", 1), ("FQ", 3), ("J", 0), ("J", 1), ("J", 3), ("GB",), ("S1",),
+    ("MR", 1, 0), ("MR", 0, 0), ("S2",), ("S3",), ("M", 2, 3), ("M", 0, 2), ("M", 1, 1), ("S4",), ("E", 1),
+    ("E", 2), ("MR", 2, 1), ("MR", 2, 0), ("rP", 1, 1), ("M", 2, 2), ("MR", 1, 2), ("rP", 0, 1), ("E", 3),
+    ("E", 0), ("rP", 1, 0), ("rP", 0, 3), ("rP", 1, 3), ("rP", 1, 2), ("rP", 0, 0), ("rCL", 1, 3),
+    ("rCL", 1, 2), ("rP", 0, 2), ("rCR", 1, 3), ("rCR", 1, 2), ("rCR", 0, 3), ("rCL", 1, 1), ("rCR", 1, 1),
+    ("rCL", 0, 3), ("MR", 0, 1), ("rCR", 0, 2), ("MR", 0, 2), ("MR", 0, 3), ("rCL", 0, 2), ("rSC", 1),
+    ("rCL", 0, 1), ("rCR", 0, 1), ("rSQ", 1), ("rSD", 1), ("rZ", 1), ("MR", 1, 1), ("rSC", 0), ("MR", 2, 2),
+    ("rFL", 1, 1), ("rFR", 1, 1), ("rSQ", 0), ("rSD", 0), ("rX", 0), ("rX", 1), ("rZ", 0), ("rFR", 1, 2),
+    ("rFL", 1, 2), ("rFR", 0, 1), ("rFL", 0, 1), ("M", 1, 3), ("rRQ", 0, 0), ("rFL", 1, 3), ("rFR", 1, 3),
+    ("rRQ", 1, 1), ("MR", 2, 3), ("rRQ", 1, 0), ("rRQ", 1, 2), ("rFR", 0, 2), ("rFR", 0, 3), ("rFL", 0, 2),
+    ("MR", 1, 3), ("rFL", 0, 3), ("rRQ", 0, 3), ("rRQ", 1, 3), ("rRQ", 0, 1), ("rRQ", 0, 2),
 )
 
 
@@ -1292,6 +1398,7 @@
             )
 
     r = Reduce(na, links, part_ref, out, scratch)
+    r.chained(scratch[9])
 
     def attend(k):
         values, probs = (
@@ -1367,7 +1474,7 @@
         shape((rows, 128), f32),
         shape((rows, quarter), f32),
     ]
-    copies = 90 + 16 * nb
+    copies = 120 + 16 * nb
     return pl.pallas_call(
         functools.partial(enter_kernel, na, nb, sizes),
         out_shape=tuple(outs),
@@ -1388,7 +1495,7 @@
             pltpu.VMEM(gu.shape, bf16),
             pltpu.VMEM(down.shape, bf16),
         ]
-        + reduce_scratch(na, rows, width)
+        + reduce_scratch(na, rows, width, True)
         + [
             pltpu.SemaphoreType.DMA((12,)),
             pltpu.SemaphoreType.DMA((copies,)),

time: 429 us -> 409 us (0.953)
  Pallas kernels: 409 us -> 388 us
    pallas_call x1, Pallas kernels: 107 us -> 91.9 us  [last_call(): pl.pallas_call(functools.partial(last_kernel, na, nb), out_shape=outs, in...]
    pallas_call x1, Pallas kernels: 156 us -> 152 us  [enter_call(): pl.pallas_call(functools.partial(enter_kernel, na, nb, sizes), out_shape=...]
where the time goes in v4:
time: 409 us; the launch traced here: 406 us
  Pallas kernels  388 us (95%)
  local copies, waits for them, and re-layouts  10.6 us (3%)
  other arithmetic  6.57 us (2%)
    pallas_call x1, Pallas kernels, enter_call(): pl.pallas_call(functools.partial(enter_kernel, na, nb, sizes), out_shape=...  152 us
    pallas_call x1, Pallas kernels, middle_call(): pl.pallas_call(functools.partial(middle_kernel, na, nb), out_shape=outs,...  145 us
    pallas_call x1, Pallas kernels, last_call(): pl.pallas_call(functools.partial(last_kernel, na, nb), out_shape=outs, in...  91.9 us

profile of v4, /device:TPU:8, one launch (start us, length us, event | category | flops | bytes accessed | tf_op | source)
XLA Modules:
  0.0 406.4 jit_solution(8897046800287036082)
XLA Ops:
  0.7 0.5 fusion
  1.2 0.8 pad_maximum_fusion
  2.0 0.8 pad_maximum_fusion.2
  2.8 0.6 broadcast_in_dim.2.refs_7_
  3.4 151.7 %enter.1 = (bf16[4,256,2048]{2,1,0:T(8,128)(2,1)}, bf16[2048,512]{1,0:T(8,128)(2,1)}, bf16[2048,1536]{1,0:T(8,128)(2,1)}, f32[8,512]{1,0:T(8,128)}, f32[8,128]{1...) custom-call(bf16[256,2048]{1,0:T(8,128)(2,1)} %refs_0_.1, ...), custom_call_target="tpu_custom_call" | custom-call | tf_op jit(solution)/shard_map/enter/pallas_call | solution.py:1478
  155.1 144.9 %middle.1 = (bf16[1,256,2048]{2,1,0:T(8,128)(2,1)}, bf16[4,256,2048]{2,1,0:T(8,128)(2,1)}, f32[8,512]{1,0:T(8,128)}, f32[256,512]{1,0:T(8,128)}, f32[8,512]{1,0:...) custom-call(bf16[4,256,2048]{2,1,0:T(8,128)(2,1)} %get-tuple-element, ...), custom_call_target="tpu_custom_call" | custom-call | tf_op jit(solution)/shard_map/middle/pallas_call | solution.py:851
  300.0 91.9 %last.1 = (bf16[1,256,2048]{2,1,0:T(8,128)(2,1)}, f32[8,640]{1,0:T(8,128)}, f32[256,2048]{1,0:T(8,128)}, f32[256,2,2048]{2,1,0:T(2,128)}, f32[3,256,512]{2,1,0:T(8,128)}, /*index=5*/f32[256,512]{1,0:T(8,128)}) custom-call(bf16[4,256,2048]{2,1,0:T(8,128)(2,1)} %get-tuple-element.44.refs_0_, bf16[4,256,2048]{2,1,0:T(8,128)(2,1)} %get-tuple-element.45.refs_1_, ...), custom_call_target="tpu_custom_call" | custom-call | tf_op jit(solution)/shard_map/last/pallas_call | solution.py:1159
  391.9 0.0 copy-start.3
  391.9 2.9 bitcast_convert_fusion
  394.8 0.8 slice.18
  395.6 0.6 fusion.2
  396.2 0.7 slice.21
  396.9 0.1 constant_dynamic-slice_fusion.1
  397.0 0.5 slice_bitcast_fusion
  397.5 0.0 copy-done.3
  397.5 1.6 bitcast_convert_fusion.1
  399.1 0.0 copy-done.2
  399.1 1.1 copy.24
  400.2 0.9 copy-done.4
  401.1 0.8 copy.25
  401.9 0.0 copy-done
  401.9 2.1 copy.26
  404.1 1.0 copy-done.1
  405.0 1.3 copy.27
  (5 shorter events, 0.0 us)
Async XLA Ops:
  391.9 5.6 %copy-start.3 = (bf16[1,256,2048]{2,1,0:T(8,128)(2,1)S(1)}, bf16[1,256,2048]{2,1,0:T(8,128)(2,1)}, u32[]{:S(2)}) copy-start(bf16[1,256,2048]{2,1,0:T(8,128)(2,1)} %get-tuple-element.43) | copy-start | bytes 3145732
  394.8 4.3 %copy-start.2 = (f32[3,256,512]{2,1,0:T(8,128)S(1)}, f32[3,256,512]{2,1,0:T(8,128)}, u32[]{:S(2)}) copy-start(f32[3,256,512]{2,1,0:T(8,128)} %get-tuple-element.59) | copy-start | bytes 4718596
  397.5 4.4 %copy-start = (f32[256,2,2048]{2,1,0:T(2,128)S(1)}, f32[256,2,2048]{2,1,0:T(2,128)}, u32[]{:S(2)}) copy-start(f32[256,2,2048]{2,1,0:T(2,128)} %get-tuple-element.86) | copy-start | bytes 12582916
  399.1 2.1 copy-start.4
  401.9 3.1 copy-start.1

commit v5 on v4

--- a/solution.py
+++ b/solution.py
@@ -882,16 +882,16 @@
 
 
 LAST = (
-    ("U1",), ("ZG", 0, 3), ("YG", 1), ("AB", 0), ("AB", 1), ("U2",), ("AB", 2), ("AB", 3),
-    ("S1",), ("WO", 1), ("U3",), ("S2",), ("WO", 2), ("S3",), ("ZG", 0, 1), ("ZG", 0, 2), ("WO", 3),
-    ("WO", 0), ("OG", 0, 3), ("S4",), ("QB", 3), ("OD", 2), ("QB", 2), ("QB", 0), ("SG", 1), ("rP", 1, 3),
-    ("ZG", 1, 2), ("QB", 1), ("ZG", 1, 3), ("rP", 1, 0), ("rP", 0, 0), ("WQ", 1), ("rP", 1, 2),
-    ("WQ", 2), ("WQ", 0), ("rP", 0, 2), ("OD", 1), ("rP", 0, 3), ("WQ", 3), ("ZG", 1, 1),
-    ("YA",), ("rP", 1, 1), ("rP", 0, 1), ("OG", 0, 1), ("rCL", 1, 3), ("rCR", 0, 3),
-    ("rCR", 1, 3), ("OG", 0, 2), ("OD", 3), ("rCL", 0, 3), ("rCR", 0, 2), ("rCR", 1, 2), ("rCL", 1, 2),
-    ("rCL", 0, 2), ("OG", 1, 1), ("OG", 1, 2), ("rCR", 0, 1), ("rCL", 1, 1), ("rCR", 1, 1), ("rCL", 0, 1),
-    ("SA",), ("ZA", 2), ("OG", 1, 3), ("ZA", 1), ("rSC", 0), ("ZA", 3), ("rSC", 1), ("rX", 0), ("U4",), ("OWNG",),
-    ("OA", 2), ("rX", 1), ("U5",), ("OWN",), ("rRQ", 0, 0), ("rRQ", 1, 0), ("OA", 1), ("OA", 3),
+    ("U1",), ("ZG", 0, 3), ("YG", 1), ("AB", 0), ("AB", 1), ("U2",), ("AB", 2), ("AB", 3), ("S1",),
+    ("WO", 1), ("U3",), ("S2",), ("WO", 2), ("S3",), ("ZG", 0, 1), ("ZG", 0, 2), ("WO", 3), ("WO", 0),
+    ("OG", 0, 3), ("S4",), ("QB", 3), ("OD", 2), ("QB", 2), ("QB", 0), ("SG", 1), ("rP", 1, 3),
+    ("ZG", 1, 2), ("QB", 1), ("ZG", 1, 3), ("rP", 1, 0), ("rP", 0, 0), ("WQ", 1), ("rP", 1, 2), ("WQ", 2),
+    ("WQ", 0), ("rP", 0, 2), ("OD", 1), ("rP", 0, 3), ("WQ", 3), ("ZG", 1, 1), ("YA",), ("OWNG",),
+    ("rP", 1, 1), ("rP", 0, 1), ("OG", 0, 1), ("rCL", 1, 3), ("rCR", 0, 3), ("rCR", 1, 3), ("OG", 0, 2),
+    ("OD", 3), ("rCL", 0, 3), ("rCR", 0, 2), ("rCR", 1, 2), ("rCL", 1, 2), ("rCL", 0, 2), ("OG", 1, 1),
+    ("OG", 1, 2), ("rCR", 0, 1), ("rCL", 1, 1), ("rCR", 1, 1), ("rCL", 0, 1), ("SA",), ("ZA", 2),
+    ("OG", 1, 3), ("ZA", 1), ("rSC", 0), ("ZA", 3), ("rSC", 1), ("rX", 0), ("U4",), ("OA", 2), ("rX", 1),
+    ("U5",), ("OWN",), ("rRQ", 0, 0), ("rRQ", 1, 0), ("OA", 1), ("OA", 3),
 )
 
 

time: 409 us -> 409 us (level)
  no operation moved by 1% of the time
where the time goes in v5:
time: 409 us; the launch traced here: 406 us
  Pallas kernels  388 us (95%)
  local copies, waits for them, and re-layouts  10.6 us (3%)
  other arithmetic  6.57 us (2%)
    pallas_call x1, Pallas kernels, enter_call(): pl.pallas_call(functools.partial(enter_kernel, na, nb, sizes), out_shape=...  152 us
    pallas_call x1, Pallas kernels, middle_call(): pl.pallas_call(functools.partial(middle_kernel, na, nb), out_shape=outs,...  145 us
    pallas_call x1, Pallas kernels, last_call(): pl.pallas_call(functools.partial(last_kernel, na, nb), out_shape=outs, in...  91.9 us

profile of v5, /device:TPU:8, one launch (start us, length us, event | category | flops | bytes accessed | tf_op | source)
XLA Modules:
  0.0 406.4 jit_solution(5050552949172914709)
XLA Ops:
  0.7 0.5 fusion
  1.2 0.8 pad_maximum_fusion
  2.0 0.8 pad_maximum_fusion.2
  2.8 0.6 broadcast_in_dim.2.refs_7_
  3.4 151.7 %enter.1 = (bf16[4,256,2048]{2,1,0:T(8,128)(2,1)}, bf16[2048,512]{1,0:T(8,128)(2,1)}, bf16[2048,1536]{1,0:T(8,128)(2,1)}, f32[8,512]{1,0:T(8,128)}, f32[8,128]{1...) custom-call(bf16[256,2048]{1,0:T(8,128)(2,1)} %refs_0_.1, ...), custom_call_target="tpu_custom_call" | custom-call | tf_op jit(solution)/shard_map/enter/pallas_call | solution.py:1478
  155.1 144.9 %middle.1 = (bf16[1,256,2048]{2,1,0:T(8,128)(2,1)}, bf16[4,256,2048]{2,1,0:T(8,128)(2,1)}, f32[8,512]{1,0:T(8,128)}, f32[256,512]{1,0:T(8,128)}, f32[8,512]{1,0:...) custom-call(bf16[4,256,2048]{2,1,0:T(8,128)(2,1)} %get-tuple-element, ...), custom_call_target="tpu_custom_call" | custom-call | tf_op jit(solution)/shard_map/middle/pallas_call | solution.py:851
  300.0 91.9 %last.1 = (bf16[1,256,2048]{2,1,0:T(8,128)(2,1)}, f32[8,640]{1,0:T(8,128)}, f32[256,2048]{1,0:T(8,128)}, f32[256,2,2048]{2,1,0:T(2,128)}, f32[3,256,512]{2,1,0:T(8,128)}, /*index=5*/f32[256,512]{1,0:T(8,128)}) custom-call(bf16[4,256,2048]{2,1,0:T(8,128)(2,1)} %get-tuple-element.44.refs_0_, bf16[4,256,2048]{2,1,0:T(8,128)(2,1)} %get-tuple-element.45.refs_1_, ...), custom_call_target="tpu_custom_call" | custom-call | tf_op jit(solution)/shard_map/last/pallas_call | solution.py:1159
  391.9 0.0 copy-start.3
  391.9 2.9 bitcast_convert_fusion
  394.8 0.8 slice.18
  395.6 0.6 fusion.2
  396.2 0.7 slice.21
  396.9 0.1 constant_dynamic-slice_fusion.1
  397.0 0.5 slice_bitcast_fusion
  397.5 0.0 copy-done.3
  397.5 1.6 bitcast_convert_fusion.1
  399.1 0.0 copy-done.2
  399.1 1.1 copy.24
  400.2 0.9 copy-done.4
  401.1 0.8 copy.25
  401.9 0.0 copy-done
  401.9 2.1 copy.26
  404.1 1.0 copy-done.1
  405.0 1.3 copy.27
  (5 shorter events, 0.0 us)
Async XLA Ops:
  391.9 5.6 %copy-start.3 = (bf16[1,256,2048]{2,1,0:T(8,128)(2,1)S(1)}, bf16[1,256,2048]{2,1,0:T(8,128)(2,1)}, u32[]{:S(2)}) copy-start(bf16[1,256,2048]{2,1,0:T(8,128)(2,1)} %get-tuple-element.43) | copy-start | bytes 3145732
  394.8 4.3 %copy-start.2 = (f32[3,256,512]{2,1,0:T(8,128)S(1)}, f32[3,256,512]{2,1,0:T(8,128)}, u32[]{:S(2)}) copy-start(f32[3,256,512]{2,1,0:T(8,128)} %get-tuple-element.59) | copy-start | bytes 4718596
  397.5 4.4 %copy-start = (f32[256,2,2048]{2,1,0:T(2,128)S(1)}, f32[256,2,2048]{2,1,0:T(2,128)}, u32[]{:S(2)}) copy-start(f32[256,2,2048]{2,1,0:T(2,128)} %get-tuple-element.86) | copy-start | bytes 12582916
  399.1 2.1 copy-start.4
  401.9 3.1 copy-start.1
